TPU v7x, 128 devices: a whole 4x4x4 slice. The times are simulated.
128 devices in a mesh: samp: 16 (over z, x), feat: 8 (over y, core).
Axes of the slice: x: 4, y: 4, z: 4, core: 2. Of those that a mesh axis runs over, the one named last changes fastest.
Arguments:
- features: bfloat16 [262144, 2048], P('samp', 'feat'), may hold values from -40 to 40
- labels: int32 [262144], P('samp'), may hold values from 0 to 9
- weights: float32 [10, 2048], P(None, 'feat'), may hold values from -6 to 6
- sketch_basis: float32 [10, 2048, 512], P(None, 'feat'), may hold values from -0.0390625 to 0.0390625
- sketch_values: float32 [512], replicated, may hold values from 0.05 to 2
Outputs:
- newton_step: float32 [10, 2048], P(None, 'feat')
All inputs are finite; a program needn't handle non-finite values.
Results may differ from a plain program's by a relative error of at most 0.001.
The roundings to bfloat16 on the way count: a program that leaves them out, or rounds other values in their place, can miss the bound.
Values may be sent and summed in bfloat16 or wider, within the bound.
A program may use at most 128 MiB of HBM per device.

v0:
```python
import math

import jax
import jax.numpy as jnp
from jax import lax
from jax.sharding import PartitionSpec as P

F = 2048
ITERS = 3


ridge = 0.05
contract_last = (((1,), (1,)), ((), ()))
contract_first = (((0,), (0,)), ((), ()))


def copy_for_each(shard, axis):
    devices = lax.axis_size(axis)
    return lax.all_to_all(
        jnp.broadcast_to(shard[None], (devices, *shard.shape)), axis, 0, 0, tiled=True
    )


def of_everyone(shard, axis):
    everything = copy_for_each(shard, axis)
    return jnp.sum(everything, axis=0)


def in_blocks(shard, dim, devices):
    before, after = (shard.shape[:dim], shard.shape[dim + 1 :])
    return jnp.moveaxis(shard.reshape(*before, devices, -1, *after), dim, 0)


def summed_on_arrival(shard, axis, dim):
    devices = lax.axis_size(axis)
    pieces = lax.all_to_all(in_blocks(shard, dim, devices), axis, 0, 0, tiled=True)
    return jnp.sum(pieces, axis=0)


def column_softmax(scores):
    column_max = jnp.max(scores, axis=0, keepdims=True)
    shifted_exp = jnp.exp(scores - column_max)
    return shifted_exp / jnp.sum(shifted_exp, axis=0, keepdims=True)


def total_one(amount):
    return of_everyone(amount, "feat")


def on_device(features, labels, weights, sketch_basis, sketch_values):
    classes, local_cols = weights.shape
    local_rows = features.shape[0]
    sketch_rank = sketch_basis.shape[2]
    samp_count = lax.axis_size("samp")
    feat_count = lax.axis_size("feat")
    total_rows = local_rows * samp_count
    row_features = lax.all_to_all(features, "feat", split_axis=0, concat_axis=1, tiled=True)
    share_rows = local_rows // feat_count
    row_start = lax.axis_index("feat") * share_rows
    own_labels = lax.dynamic_slice_in_dim(labels, row_start, share_rows, 0)
    onehot = (own_labels[None, :] == jnp.arange(classes, dtype=jnp.int32)[:, None]).astype(
        jnp.float32
    )

    def class_logits(rounded):
        partial_logits = lax.dot_general(
            rounded, row_features, contract_last, preferred_element_type=jnp.float32
        )
        return partial_logits

    def feature_sums(coeffs):
        coeffs_b = coeffs.astype(jnp.bfloat16)
        whole_cols = jnp.dot(coeffs_b, row_features, preferred_element_type=jnp.float32)
        partial_cols = summed_on_arrival(whole_cols, "feat", 1)
        return of_everyone(partial_cols, "samp")

    weights_b = weights.astype(jnp.bfloat16)
    weights_b = lax.all_gather(weights_b, "feat", axis=1, tiled=True)
    probabilities = column_softmax(class_logits(weights_b) / math.sqrt(F))
    gradient = feature_sums(probabilities - onehot) * (math.sqrt(F) / total_rows) + ridge * weights
    flat_local = sketch_basis.reshape(classes * local_cols, sketch_rank)
    local_gram = lax.dot_general(
        flat_local, flat_local, contract_first, precision=lax.Precision.HIGHEST
    )
    gram_matrix = lax.psum(local_gram, "feat")
    factor = jnp.linalg.cholesky(gram_matrix)
    coefficients = (jnp.min(sketch_values) + ridge) / (sketch_values + ridge) - 1.0
    basis_own = sketch_basis.reshape(classes * local_cols, sketch_rank)

    def precondition(residue):
        local_proj = jnp.dot(residue.reshape(-1), basis_own, precision=lax.Precision.HIGHEST)
        projection = total_one(local_proj)
        inner_coords = jax.scipy.linalg.solve_triangular(factor, projection, lower=True)
        weighted_coords = coefficients * inner_coords
        outer_coords = jax.scipy.linalg.solve_triangular(
            factor, weighted_coords, lower=True, trans=1
        )
        scaled_res = residue + jnp.dot(
            basis_own, outer_coords, precision=lax.Precision.HIGHEST
        ).reshape(residue.shape)
        return (scaled_res, total_one(jnp.sum(residue * scaled_res)))

    residue = -gradient
    newton_part = jnp.zeros_like(residue)
    scaled_res, res_dot = precondition(residue)
    direction = scaled_res
    for iteration in range(ITERS):
        hessian_rounded = direction.astype(jnp.bfloat16)
        gathered = hessian_rounded
        gathered = lax.all_gather(gathered, "feat", axis=1, tiled=True)
        image_vals = class_logits(gathered)
        weighted = probabilities * image_vals
        curvature = weighted - probabilities * jnp.sum(weighted, axis=0, keepdims=True)
        hess_image = feature_sums(curvature) / total_rows + ridge * direction
        step_size = res_dot / total_one(jnp.sum(direction * hess_image))
        newton_part = newton_part + step_size * direction
        if iteration + 1 < ITERS:
            residue = residue - step_size * hess_image
            scaled_res, new_dot = precondition(residue)
            direction = scaled_res + new_dot / res_dot * direction
            res_dot = new_dot
    return newton_part


def solution(mesh):
    in_specs = (P("samp", "feat"), P("samp"), P(None, "feat"), P(None, "feat", None), P())
    out_specs = P(None, "feat")
    return jax.shard_map(
        on_device, mesh=mesh, in_specs=in_specs, out_specs=out_specs, check_vma=False
    )
```

profile of v0, /device:TPU:1, one launch (start us, length us, event | category | flops | bytes accessed | tf_op | source)
XLA Modules:
  0.0 570.1 jit_solution(3799169834706363901)
XLA Ops:
  6.5 6.3 %all-to-all-start = ((bf16[8,2048,256]{2,1,0:T(8,128)(2,1)}), bf16[8,2048,256]{2,1,0:T(8,128)(2,1)}, u32[]{:S(2)}, u32[]{:S(2)}) async-start(bf16[8,2048,256]{2,1,0:T(8,128)(2,1)} %bitcast.495), calls=%async_computation | async-start | bytes 16777216 | tf_op jit(solution)/shard_map/all_to_all | solution.py:57
  12.9 12.3 %convolution_bitcast_fusion = f32[512,512]{0,1:T(8,128)} fusion(f32[10,256,512]{2,1,0:T(8,128)} %param.12), kind=kOutput, calls=%fused_computation.14 | convolution fusion | flops 8053063680 | bytes 6291456 | tf_op jit(solution)/shard_map/dot_general | solution.py:82
  26.5 96.5 %all_gather.12 = bf16[10,2048]{1,0:T(8,128)(2,1)S(1)} all-gather(bf16[10,256]{1,0:T(8,128)(2,1)S(1)} %convert_element_type.27), channel_id=1, replica_groups=mesh['samp'=16,'feat'=8] {'feat'}, dimensions={1}, use_global_device_ids=true | all-gather | bytes 46080 | tf_op jit(solution)/shard_map/all_gather | solution.py:78
  123.0 1.6 copy.18
  124.6 1.4 fusion.56
  126.0 11.7 %cholesky.104 = f32[128,128]{1,0:T(8,128)S(1)} custom-call(f32[128,128]{1,0:T(8,128)S(1)} %cholesky.266), custom_call_target="Cholesky" | custom-call | tf_op jit(solution)/shard_map/jit(cholesky)/cholesky | solution.py:86
  137.9 9.8 %custom-call.33 = f32[1,128,128]{1,2,0:T(8,128)S(1)} custom-call(f32[1,128,128]{2,1,0:T(8,128)S(1)} %get-tuple-element.78), custom_call_target="InvertDiagBlocksLowerTriangular" | custom-call | tf_op jit(solution)/shard_map/jit(cholesky)/cholesky | solution.py:86
  148.4 11.7 %cholesky.217 = f32[128,128]{1,0:T(8,128)S(1)} custom-call(f32[128,128]{1,0:T(8,128)S(1)} %cholesky.270), custom_call_target="Cholesky" | custom-call | tf_op jit(solution)/shard_map/jit(cholesky)/cholesky | solution.py:86
  160.1 10.0 %custom-call.34 = f32[1,128,128]{1,2,0:T(8,128)S(1)} custom-call(f32[1,128,128]{2,1,0:T(8,128)S(1)} %get-tuple-element.75), custom_call_target="InvertDiagBlocksLowerTriangular" | custom-call | tf_op jit(solution)/shard_map/jit(cholesky)/cholesky | solution.py:86
  170.8 11.7 %cholesky.238 = f32[128,128]{1,0:T(8,128)S(1)} custom-call(f32[128,128]{1,0:T(8,128)S(1)} %cholesky.275), custom_call_target="Cholesky" | custom-call | tf_op jit(solution)/shard_map/jit(cholesky)/cholesky | solution.py:86
  182.6 9.8 %custom-call.35 = f32[1,128,128]{1,2,0:T(8,128)S(1)} custom-call(f32[1,128,128]{2,1,0:T(8,128)S(1)} %get-tuple-element.72), custom_call_target="InvertDiagBlocksLowerTriangular" | custom-call | tf_op jit(solution)/shard_map/jit(cholesky)/cholesky | solution.py:86
  193.0 12.1 %cholesky.255 = f32[128,128]{1,0:T(8,128)S(1)} custom-call(f32[128,128]{1,0:T(8,128)S(1)} %convolution_subtract_fusion.2), custom_call_target="Cholesky" | custom-call | tf_op jit(solution)/shard_map/jit(cholesky)/cholesky | solution.py:86
  205.1 0.7 compare_reduce_fusion.2
  207.0 0.7 compare_reduce_fusion.1
  208.5 11.6 %copy.14 = bf16[2048,8,256]{0,2,1:T(8,128)(2,1)} copy(bf16[2048,8,256]{2,0,1:T(8,128)(2,1)} %bitcast.1) | data formatting | bytes 16777216 | tf_op jit(solution)/shard_map/all_to_all | solution.py:57
  220.1 4.7 fusion.221
  224.9 1.1 slice-done.1
  225.9 2.9 fusion.8
  228.9 3.5 all-to-all-start.1
  233.7 4.0 all-to-all-done.1
  237.6 0.7 broadcast_in_dim.30
  238.4 7.7 %all-to-all-start.2 = ((f32[16,10,256]{2,1,0:T(8,128)}), f32[16,10,256]{2,1,0:T(8,128)S(1)}, u32[]{:S(2)}, u32[]{:S(2)}) async-start(f32[16,10,256]{2,1,0:T(8,128)} %broadcast_in_dim.30), calls=%async_computation.2 | async-start | bytes 524288 | tf_op jit(solution)/shard_map/all_to_all | solution.py:19
  246.2 7.4 %all-to-all-done.2 = f32[16,10,256]{2,1,0:T(8,128)S(1)} async-done(((f32[16,10,256]{2,1,0:T(8,128)}), f32[16,10,256]{2,1,0:T(8,128)S(1)}, u32[]{:S(2)}, u32[]{:S(2)}) %all-to-all-start.2) | async-done | bytes 163872 | tf_op jit(solution)/shard_map/all_to_all | solution.py:19
  253.7 5.0 fusion.110
  259.4 5.7 all-to-all-start.3
  265.1 10.0 %while.12 = (s32[]{:T(128)}, f32[512,512]{1,0:T(8,128)S(1)}, s32[4,2]{0,1:T(2,128)S(1)}, f32[4,128,128]{2,1,0:T(8,128)}, s32[]{:T(128)}) while((s32[]{:T(128)}, f32[512,512]{1,0:T(8,128)S(1)}, s32[4,2]{0,1:T(2,128)S(1)}, f32[4,128,128]{2,1,0:T(8,128)}, s32[]{:T(128)}) %tuple.53), condition=%wide.while_cond.1, body=%wide.while_body.1.sunk | while | flops 2 | bytes 132205 | solution.py:95
  265.7 1.9 bitcast_dynamic-update-slice_fusion.2
  268.2 1.9 bitcast_dynamic-update-slice_fusion.2
  270.7 1.9 bitcast_dynamic-update-slice_fusion.2
  273.2 1.9 bitcast_dynamic-update-slice_fusion.2
  275.1 40.1 %custom-call.41 = f32[4,128,128]{1,2,0:T(8,128)S(1)} custom-call(f32[4,128,128]{2,1,0:T(8,128)} %get-tuple-element.48), custom_call_target="InvertDiagBlocksLowerTriangular" | custom-call | tf_op jit(solution)/shard_map/jit(_solve_triangular)/triangular_solve | solution.py:95
  318.3 6.8 %fusion.112 = f32[1,10,256]{2,0,1:T(1,128)S(1)} fusion(f32[10,256,512]{2,1,0:T(8,128)} %param.12, f32[128,1]{0,1:T(1,128)S(1)} %convolution_bitcast_fusion.30, f32[128,1]{0,1:T(1,128)S(1)} %convolution_bitcast_fusion.28, f32[128,1]{0,1:T(1,128)S(1)} %convolution_bitcast_fusion.26, f32[128,1]{0,1:T(1,128)S(1)} %convolution_bitcast_fusion.25), kind=kOutput, calls=%fused_computation.191 | convolution fusion | flops 15730176 | bytes 5255168 | tf_op jit(solution)/shard_map/dot_general | solution.py:98
  325.1 13.6 %all_gather.13 = bf16[10,2048]{1,0:T(8,128)(2,1)S(1)} all-gather(bf16[10,256]{1,0:T(8,128)(2,1)S(1)} %fusion.208), channel_id=1, replica_groups=mesh['samp'=16,'feat'=8] {'feat'}, dimensions={1}, use_global_device_ids=true | all-gather | bytes 46080 | tf_op jit(solution)/shard_map/all_gather | solution.py:110
  338.7 4.7 fusion.222
  343.5 2.3 fusion.11
  345.8 8.8 %all_to_all.113 = f32[8,10,256]{2,1,0:T(8,128)S(1)} all-to-all(f32[8,10,256]{2,1,0:T(8,128)S(1)} %fusion.11), channel_id=1, replica_groups=mesh['samp'=16,'feat'=8] {'feat'}, dimensions={0} | all-to-all | bytes 163840 | tf_op jit(solution)/shard_map/all_to_all | solution.py:36
  354.7 10.2 %all_to_all.114 = f32[16,10,256]{2,1,0:T(8,128)S(1)} all-to-all(f32[16,10,256]{2,1,0:T(8,128)S(1)} %broadcast_in_dim.33), channel_id=1, replica_groups=mesh['samp'=16,'feat'=8] {'samp'}, dimensions={0} | all-to-all | bytes 327680 | tf_op jit(solution)/shard_map/all_to_all | solution.py:19
  365.5 0.6 broadcast_in_dim.32
  366.2 9.2 %all_to_all.115 = f32[8,1,1]{2,1,0:T(1,128)S(1)} all-to-all(f32[8,1,1]{2,1,0:T(1,128)S(1)} %broadcast_in_dim.32), channel_id=1, replica_groups=mesh['samp'=16,'feat'=8] {'feat'}, dimensions={0} | all-to-all | bytes 64 | tf_op jit(solution)/shard_map/all_to_all | solution.py:19
  375.4 1.2 broadcast_in_dim.34
  376.5 4.1 all-to-all-start.7
  381.3 3.9 all-to-all-done.7
  387.1 5.0 fusion.108
  392.2 7.7 %all_to_all.116 = f32[8,1,512]{2,1,0:T(1,128)S(1)} all-to-all(f32[8,1,512]{2,1,0:T(1,128)S(1)} %broadcast_in_dim.35), channel_id=1, replica_groups=mesh['samp'=16,'feat'=8] {'feat'}, dimensions={0} | all-to-all | bytes 32768 | tf_op jit(solution)/shard_map/all_to_all | solution.py:19
  402.9 6.8 %fusion.119 = f32[1,10,256]{2,0,1:T(1,128)S(1)} fusion(f32[10,256,512]{2,1,0:T(8,128)} %param.12, f32[128,1]{0,1:T(1,128)S(1)} %convolution_bitcast_fusion.18, f32[128,1]{0,1:T(1,128)S(1)} %convolution_bitcast_fusion.16, f32[128,1]{0,1:T(1,128)S(1)} %convolution_bitcast_fusion.14, f32[128,1]{0,1:T(1,128)S(1)} %convolution_bitcast_fusion.13), kind=kOutput, calls=%fused_computation.200 | convolution fusion | flops 15730176 | bytes 5255168 | tf_op jit(solution)/shard_map/dot_general | solution.py:98
  410.3 0.6 broadcast_in_dim.36
  411.0 7.7 %all_to_all.117 = f32[8,1,1]{2,1,0:T(1,128)S(1)} all-to-all(f32[8,1,1]{2,1,0:T(1,128)S(1)} %broadcast_in_dim.36), channel_id=1, replica_groups=mesh['samp'=16,'feat'=8] {'feat'}, dimensions={0} | all-to-all | bytes 64 | tf_op jit(solution)/shard_map/all_to_all | solution.py:19
  420.5 13.3 %all_gather.14 = bf16[10,2048]{1,0:T(8,128)(2,1)S(1)} all-gather(bf16[10,256]{1,0:T(8,128)(2,1)S(1)} %get-tuple-element.65), channel_id=1, replica_groups=mesh['samp'=16,'feat'=8] {'feat'}, dimensions={1}, use_global_device_ids=true | all-gather | bytes 46080 | tf_op jit(solution)/shard_map/all_gather | solution.py:110
  433.8 4.6 fusion.223
  438.4 5.6 fusion.14
  444.1 7.9 %all_to_all.118 = f32[8,10,256]{2,1,0:T(8,128)S(1)} all-to-all(f32[8,10,256]{2,1,0:T(8,128)S(1)} %fusion.14), channel_id=1, replica_groups=mesh['samp'=16,'feat'=8] {'feat'}, dimensions={0} | all-to-all | bytes 163840 | tf_op jit(solution)/shard_map/all_to_all | solution.py:36
  452.1 10.2 %all_to_all.119 = f32[16,10,256]{2,1,0:T(8,128)S(1)} all-to-all(f32[16,10,256]{2,1,0:T(8,128)S(1)} %broadcast_in_dim.37), channel_id=1, replica_groups=mesh['samp'=16,'feat'=8] {'samp'}, dimensions={0} | all-to-all | bytes 327680 | tf_op jit(solution)/shard_map/all_to_all | solution.py:19
  463.4 9.5 %all_to_all.120 = f32[8,1,1]{2,1,0:T(1,128)S(1)} all-to-all(f32[8,1,1]{2,1,0:T(1,128)S(1)} %broadcast_in_dim.38), channel_id=1, replica_groups=mesh['samp'=16,'feat'=8] {'feat'}, dimensions={0} | all-to-all | bytes 64 | tf_op jit(solution)/shard_map/all_to_all | solution.py:19
  474.8 5.0 fusion.106
  479.8 7.7 %all_to_all.121 = f32[8,1,512]{2,1,0:T(1,128)S(1)} all-to-all(f32[8,1,512]{2,1,0:T(1,128)S(1)} %broadcast_in_dim.39), channel_id=1, replica_groups=mesh['samp'=16,'feat'=8] {'feat'}, dimensions={0} | all-to-all | bytes 32768 | tf_op jit(solution)/shard_map/all_to_all | solution.py:19
  490.5 6.8 %fusion.126 = f32[1,10,256]{2,0,1:T(1,128)S(1)} fusion(f32[10,256,512]{2,1,0:T(8,128)} %param.12, f32[128,1]{0,1:T(1,128)S(1)} %convolution_bitcast_fusion.6, f32[128,1]{0,1:T(1,128)S(1)} %convolution_bitcast_fusion.4, f32[128,1]{0,1:T(1,128)S(1)} %convolution_bitcast_fusion.2, f32[128,1]{0,1:T(1,128)S(1)} %convolution_bitcast_fusion.1), kind=kOutput, calls=%fused_computation.209 | convolution fusion | flops 15730176 | bytes 5255168 | tf_op jit(solution)/shard_map/dot_general | solution.py:98
  498.5 7.7 %all_to_all.122 = f32[8,1,1]{2,1,0:T(1,128)S(1)} all-to-all(f32[8,1,1]{2,1,0:T(1,128)S(1)} %broadcast_in_dim.40), channel_id=1, replica_groups=mesh['samp'=16,'feat'=8] {'feat'}, dimensions={0} | all-to-all | bytes 64 | tf_op jit(solution)/shard_map/all_to_all | solution.py:19
  508.1 13.3 %all_gather.15 = bf16[10,2048]{1,0:T(8,128)(2,1)S(1)} all-gather(bf16[10,256]{1,0:T(8,128)(2,1)S(1)} %get-tuple-element.63), channel_id=1, replica_groups=mesh['samp'=16,'feat'=8] {'feat'}, dimensions={1}, use_global_device_ids=true | all-gather | bytes 46080 | tf_op jit(solution)/shard_map/all_gather | solution.py:110
  521.4 4.6 fusion.224
  526.0 5.6 fusion.17
  531.6 7.9 %all_to_all.123 = f32[8,10,256]{2,1,0:T(8,128)S(1)} all-to-all(f32[8,10,256]{2,1,0:T(8,128)S(1)} %fusion.17), channel_id=1, replica_groups=mesh['samp'=16,'feat'=8] {'feat'}, dimensions={0} | all-to-all | bytes 163840 | tf_op jit(solution)/shard_map/all_to_all | solution.py:36
  539.6 10.2 %all_to_all.124 = f32[16,10,256]{2,1,0:T(8,128)S(1)} all-to-all(f32[16,10,256]{2,1,0:T(8,128)S(1)} %broadcast_in_dim.41), channel_id=1, replica_groups=mesh['samp'=16,'feat'=8] {'samp'}, dimensions={0} | all-to-all | bytes 327680 | tf_op jit(solution)/shard_map/all_to_all | solution.py:19
  550.4 0.6 broadcast_in_dim.42
  551.1 9.2 %all_to_all.125 = f32[8,1,1]{2,1,0:T(1,128)S(1)} all-to-all(f32[8,1,1]{2,1,0:T(1,128)S(1)} %broadcast_in_dim.42), channel_id=1, replica_groups=mesh['samp'=16,'feat'=8] {'feat'}, dimensions={0} | all-to-all | bytes 64 | tf_op jit(solution)/shard_map/all_to_all | solution.py:19
  (135 shorter events, 24.2 us)
Async XLA Ops:
  6.5 201.9 %all-to-all-start = ((bf16[8,2048,256]{2,1,0:T(8,128)(2,1)}), bf16[8,2048,256]{2,1,0:T(8,128)(2,1)}, u32[]{:S(2)}, u32[]{:S(2)}) async-start(bf16[8,2048,256]{2,1,0:T(8,128)(2,1)} %bitcast.495), calls=%async_computation | async-start | bytes 16777216 | tf_op jit(solution)/shard_map/all_to_all | solution.py:57
  12.8 12.4 %copy-start = (f32[10,256]{1,0:T(8,128)S(1)}, f32[10,256]{1,0:T(8,128)}, u32[]{:S(2)}) copy-start(f32[10,256]{1,0:T(8,128)} %param.11) | copy-start | bytes 30724
  12.8 12.4 %copy-start.1 = (f32[512]{0:T(512)S(1)}, f32[512]{0:T(512)}, u32[]{:S(2)}) copy-start(f32[512]{0:T(512)} %param.13) | copy-start | bytes 6148
  12.8 110.2 %all-reduce.3.cloned.1.call-start = ((), (), s32[]{:S(2)}) async-start(), calls=%async_computation.18 | async-start | bytes 2097152 | tf_op jit(solution)/shard_map/psum | solution.py:85
  220.1 4.8 slice-start
  220.1 4.8 dynamic-slice-start
  220.1 5.9 %slice-start.1 = ((s8[8388608]{0:T(1024)(128)(4,1)}), s8[4194304]{0:T(1024)(128)(4,1)S(1)}, s32[]{:S(2)}) async-start(s8[8388608]{0:T(1024)(128)(4,1)} %bitcast.491), calls=%async_computation.20 | async-start | bytes 8388608
  228.9 8.8 %all-to-all-start.1 = ((f32[8,10,256]{2,1,0:T(8,128)}), f32[8,10,256]{2,1,0:T(8,128)S(1)}, u32[]{:S(2)}, u32[]{:S(2)}) async-start(f32[8,10,256]{2,1,0:T(8,128)} %fusion.8), calls=%async_computation.1 | async-start | bytes 262144 | tf_op jit(solution)/shard_map/all_to_all | solution.py:36
  238.4 15.3 %all-to-all-start.2 = ((f32[16,10,256]{2,1,0:T(8,128)}), f32[16,10,256]{2,1,0:T(8,128)S(1)}, u32[]{:S(2)}, u32[]{:S(2)}) async-start(f32[16,10,256]{2,1,0:T(8,128)} %broadcast_in_dim.30), calls=%async_computation.2 | async-start | bytes 524288 | tf_op jit(solution)/shard_map/all_to_all | solution.py:19
  259.4 55.9 %all-to-all-start.3 = ((f32[8,1,512]{2,1,0:T(1,128)}), f32[8,1,512]{2,1,0:T(1,128)S(1)}, u32[]{:S(2)}, u32[]{:S(2)}) async-start(f32[8,1,512]{2,1,0:T(1,128)} %broadcast_in_dim.31), calls=%async_computation.3 | async-start | bytes 32768 | tf_op jit(solution)/shard_map/all_to_all | solution.py:19
  325.1 18.4 %slice-start.2 = ((s8[8388608]{0:T(1024)(128)(4,1)}), s8[4194304]{0:T(1024)(128)(4,1)S(1)}, s32[]{:S(2)}) async-start(s8[8388608]{0:T(1024)(128)(4,1)} %bitcast.493), calls=%async_computation.21 | async-start | bytes 8388608
  338.7 4.8 slice-start.3
  376.5 8.7 %all-to-all-start.7 = ((f32[8,1,1]{2,1,0:T(1,128)}), f32[8,1,1]{2,1,0:T(1,128)S(1)}, u32[]{:S(2)}, u32[]{:S(2)}) async-start(f32[8,1,1]{2,1,0:T(1,128)} %broadcast_in_dim.34), calls=%async_computation.7 | async-start | bytes 8192 | tf_op jit(solution)/shard_map/all_to_all | solution.py:19
Sparse Core Ops, SparseCore 0:
  25.3 71.8 all-reduce.2
where the time goes:
time: 576 us; the launch traced here: 570 us
  blocking collectives  251 us (44%)
  other arithmetic  129 us (22%)
  matrix products  93.6 us (16%)
  local copies, waits for them, and re-layouts  30.1 us (5%)
  starting transfers between devices  27.4 us (5%)
  between operations  23.9 us (4%)
  waiting for transfers between devices  15.4 us (3%)
    all_gather x1, blocking collectives, on_device(): weights_b = lax.all_gather(weights_b, 'feat', axis=1, tiled=True)  96.5 us
    all_to_all x10, blocking collectives, copy_for_each(): lax.all_to_all(jnp.broadcast_to(shard[None], (devices, *shard.shape)), ax...  89.3 us
    another operation x14, other arithmetic, on_device(): factor = jnp.linalg.cholesky(gram_matrix)  79 us
    another operation x4, other arithmetic, precondition(): jax.scipy.linalg.solve_triangular(factor, weighted_coords, lower=True, tr...  40.3 us
    all_gather x3, blocking collectives, on_device(): gathered = lax.all_gather(gathered, 'feat', axis=1, tiled=True)  40.2 us
    all_to_all x3, blocking collectives, summed_on_arrival(): lax.all_to_all(in_blocks(shard, dim, devices), axis, 0, 0, tiled=True)  24.7 us
    dot_general x3, matrix products, precondition(): jnp.dot(basis_own, outer_coords, precision=lax.Precision.HIGHEST)  20.5 us
    dot_general x4, matrix products, class_logits(): lax.dot_general(rounded, row_features, contract_last, preferred_element_t...  18.7 us
  transfers between devices with their start and end apart: 6, of which 3 were waited for; matrix products, arithmetic and copies ran while one was open for 26% of the time, Pallas kernels for 0%

commit v1 on v0

v1 whole, which is shorter than its diff:
```python
import functools
import math

import jax
import jax.numpy as jnp
from jax import lax
from jax.experimental import pallas as pl
from jax.experimental.pallas import tpu as pltpu
from jax.sharding import PartitionSpec as P

F = 2048
ITERS = 3
RIDGE = 0.05
SAMP, YS, CORES = 16, 4, 2
FEAT = YS * CORES
ROWS = 16384
HALF = ROWS // CORES
CHUNKS = 4
CROWS = HALF // CHUNKS
PIECE = CROWS // YS
COLS = 256
K = 10
RANK = 512
LT = K * COLS // 128
f32, bf16 = jnp.float32, jnp.bfloat16
HI = lax.Precision.HIGHEST
NT = (((1,), (1,)), ((), ()))
TN = (((0,), (0,)), ((), ()))


def rcopy(src, dst, send, recv, dev):
    return pltpu.make_async_remote_copy(
        src_ref=src, dst_ref=dst, send_sem=send, recv_sem=recv,
        device_id=dev, device_id_type=pl.DeviceIdType.MESH,
    )


def rows_of(n):
    return lax.broadcasted_iota(jnp.int32, (n, 128), 0)


def pack(wide):
    low = wide[8:16]
    third = low[:, :128] + pltpu.roll(low[:, 128:], 2, 0)
    return jnp.concatenate([wide[:8], third], axis=1)


def unpack(packed):
    third = packed[:, 256:]
    row = rows_of(8)
    left = jnp.where(row < 2, third, 0.0)
    right = jnp.where(row < 2, pltpu.roll(third, 6, 0), 0.0)
    return jnp.concatenate([packed[:, :256], jnp.concatenate([left, right], axis=1)], axis=0)


def lane_row(packed, k, h):
    if k < 8:
        return packed[k : k + 1, h * 128 : (h + 1) * 128]
    r = 2 * h + (k - 8)
    return packed[r : r + 1, 256:384]


def column(row):
    return jnp.broadcast_to(row, (128, 128)).T


def factor_block(A, N):
    for p in range(16):
        lo = 8 * p
        n = 128 - lo
        ap = A[lo:128, :]
        cols = [jnp.broadcast_to(ap[:, lo + j : lo + j + 1], (n, 128)) for j in range(8)]
        arow, nrow = A[lo : lo + 8, :], N[lo : lo + 8, :]
        cs, us, ns = [], [], []
        for j in range(8):
            r = lax.rsqrt(cols[j][j : j + 1, :])
            c = cols[j] * r
            u = arow[j : j + 1, :] * r
            v = nrow[j : j + 1, :] * r
            for k in range(j + 1, 8):
                cols[k] = cols[k] - c * c[k : k + 1, :]
            arow = arow - c[:8] * u
            nrow = nrow - c[:8] * v
            cs.append(c)
            us.append(u)
            ns.append(v)
        if n > 8:
            at, nt = A[lo + 8 : 128, :], N[lo + 8 : 128, :]
            for j in range(8):
                at = at - cs[j][8:] * us[j]
                nt = nt - cs[j][8:] * ns[j]
            A[lo + 8 : 128, :] = at
            N[lo + 8 : 128, :] = nt
        N[lo : lo + 8, :] = jnp.concatenate(ns, axis=0)


def kernel(
    feat, labels, w16, basis, svals, out,
    X, bst, BT, dB, imgf, imgb, recvg, recvh, prob, E, Q, Qr, ar, fe,
    gparts, gall, V, AK, FA, FN, ccol, tmp, vec, prow, scal,
    sx_own, sx_s, sx_r, s_b, rs_s, rs_r, ag_s, ag_r, q_s, q_r, d_s, d_r,
    ar_s, ar_r, fe_s, fe_r, gf_s, gf_r, gs_s, gs_r,
):
    s = lax.axis_index("samp")
    f = lax.axis_index("feat")
    y = lax.div(f, CORES)
    c = lax.rem(f, CORES)
    sib = (s, f + 1 - 2 * c)

    def samp_dev(i):
        return lax.rem(s + i, SAMP)

    def feat_dev(i):
        return lax.rem(f + i, FEAT)

    def y_dev(i):
        return lax.rem(y + i, YS)

    for k in range(K):
        pltpu.make_async_copy(basis.at[pl.ds(k * COLS, COLS)], bst.at[pl.ds(k * COLS, COLS)], s_b.at[k]).start()

    def own_rows(t):
        return pl.ds(pl.multiple_of(c * HALF + t * CROWS, CROWS), CROWS)

    def sib_rows(t):
        return pl.ds(pl.multiple_of((1 - c) * HALF + t * CROWS, CROWS), CROWS)

    def x_own(t):
        return pltpu.make_async_copy(feat.at[own_rows(t)], X.at[c, pl.ds(t * CROWS, CROWS)], sx_own.at[t])

    def x_send(t):
        return rcopy(feat.at[sib_rows(t)], X.at[c, pl.ds(t * CROWS, CROWS)], sx_s.at[t], sx_r.at[t], sib)

    def x_recv(t):
        dst = X.at[1 - c, pl.ds(t * CROWS, CROWS)]
        return rcopy(dst, dst, sx_s.at[t], sx_r.at[t], sib)

    for t in range(CHUNKS):
        x_own(t).start()

    def d_copy(ph):
        return rcopy(dB.at[ph, c], dB.at[ph, c], d_s.at[ph], d_r.at[ph], sib)

    def d_recv(ph):
        return rcopy(dB.at[ph, 1 - c], dB.at[ph, 1 - c], d_s.at[ph], d_r.at[ph], sib)

    barrier = pltpu.get_barrier_semaphore()
    for i in range(1, FEAT):
        pl.semaphore_signal(barrier, inc=1, device_id=(s, feat_dev(i)), device_id_type=pl.DeviceIdType.MESH)
    for i in range(1, SAMP):
        pl.semaphore_signal(barrier, inc=1, device_id=(samp_dev(i), f), device_id_type=pl.DeviceIdType.MESH)

    w = w16[...]
    dB[0, c] = w.astype(bf16)
    pl.semaphore_wait(barrier, FEAT - 1 + SAMP - 1)
    d_copy(0).start()
    for t in range(CHUNKS):
        x_send(t).start()

    @pl.loop(0, K)
    def _(k):
        pltpu.make_async_copy(
            basis.at[pl.ds(k * COLS, COLS)], bst.at[pl.ds(k * COLS, COLS)], s_b.at[k]
        ).wait()
        for h in range(2):
            for jt in range(4):
                blk = bst[pl.ds(pl.multiple_of(k * COLS + h * 128, 128), 128), jt * 128 : (jt + 1) * 128]
                BT[jt * 128 : (jt + 1) * 128, pl.ds(pl.multiple_of(k * COLS + h * 128, 128), 128)] = blk.T

    blk_id = lax.min(s, 9)
    ba = sum((blk_id >= e).astype(jnp.int32) for e in (4, 7, 9))
    bb = blk_id - lax.div(ba * (9 - ba), 2) + ba

    def gram_step(kk, acc):
        cols = pl.ds(pl.multiple_of(kk * 256, 256), 256)
        return acc + lax.dot_general(
            BT[pl.ds(pl.multiple_of(ba * 128, 128), 128), cols],
            BT[pl.ds(pl.multiple_of(bb * 128, 128), 128), cols],
            NT, precision=HI, preferred_element_type=f32,
        )

    gparts[f] = lax.fori_loop(0, K, gram_step, jnp.zeros((128, 128), f32))

    def gf_copy(i):
        return rcopy(gparts.at[f], gparts.at[f], gf_s.at[i], gf_r.at[f], (s, feat_dev(i)))

    def gf_recv(i):
        src = feat_dev(i)
        return rcopy(gparts.at[src], gparts.at[src], gf_s.at[i], gf_r.at[src], (s, src))

    def gs_copy(i):
        return rcopy(gall.at[s], gall.at[s], gs_s.at[i], gs_r.at[s], (samp_dev(i), f))

    @pl.when(s < 10)
    def _():
        for i in range(1, FEAT):
            gf_copy(i).start()

    def rs_copy(ph, t, i, grad):
        o = y_dev(i)
        src = imgf.at[t, o] if grad else imgb.at[t, o]
        dst = recvg.at[t, y] if grad else recvh.at[ph - 1, t, y]
        return rcopy(src, dst, rs_s.at[ph, t, i], rs_r.at[ph, t, y], (s, CORES * o + c))

    def rs_recv(ph, t, i, grad):
        o = y_dev(i)
        dst = recvg.at[t, o] if grad else recvh.at[ph - 1, t, o]
        return rcopy(dst, dst, rs_s.at[ph, t, i], rs_r.at[ph, t, o], (s, CORES * o + c))

    def ag_copy(ph, t, i):
        return rcopy(E.at[ph, t, y], E.at[ph, t, y], ag_s.at[ph, t, i], ag_r.at[ph, t, y], (s, CORES * y_dev(i) + c))

    def ag_recv(ph, t, i):
        o = y_dev(i)
        return rcopy(E.at[ph, t, o], E.at[ph, t, o], ag_s.at[ph, t, i], ag_r.at[ph, t, o], (s, CORES * o + c))

    def images(ph, grad):
        @pl.loop(0, CHUNKS)
        def _(t):
            if grad:
                x_own(t).wait()
                x_recv(t).wait_recv()
            at = pl.ds(pl.multiple_of(t * CROWS, CROWS), CROWS)
            img = lax.dot_general(dB[ph, 0], X[0, at], NT, preferred_element_type=f32)
            img = img + lax.dot_general(dB[ph, 1], X[1, at], NT, preferred_element_type=f32)
            for o in range(YS):
                piece = img[:, o * PIECE : (o + 1) * PIECE]
                imgf[t, o] = piece
                if not grad:
                    imgb[t, o] = piece.astype(bf16)
            for i in range(1, YS):
                rs_copy(ph, t, i, grad).start()

    def pieces(ph, grad):
        @pl.loop(0, CHUNKS)
        def _(t):
            total = imgf[t, y]
            for i in range(1, YS):
                rs_recv(ph, t, i, grad).wait_recv()
            for i in range(1, YS):
                o = y_dev(i)
                total = total + (recvg[t, o] if grad else recvh[ph - 1, t, o].astype(f32))
            if grad:
                logits = total / math.sqrt(F)
                row = lax.broadcasted_iota(jnp.int32, (16, PIECE), 0)
                logits = jnp.where(row < K, logits, -jnp.inf)
                top = jnp.max(logits, axis=0, keepdims=True)
                ex = jnp.exp(logits - top)
                pr = ex / jnp.sum(ex, axis=0, keepdims=True)
                prob[t] = pr
                own = labels[pl.ds(c * (CHUNKS * YS) + t * YS + y, 1), :]
                coeffs = pr - jnp.where(row == own, 1.0, 0.0)
            else:
                pr = prob[t]
                weighted = pr * total
                coeffs = weighted - pr * jnp.sum(weighted, axis=0, keepdims=True)
            E[ph, t, y] = coeffs.astype(bf16)
            for i in range(1, YS):
                ag_copy(ph, t, i).start()

    def collect(ph):
        Q[...] = jnp.zeros_like(Q)

        @pl.loop(0, CHUNKS)
        def _(t):
            for i in range(1, YS):
                ag_recv(ph, t, i).wait_recv()
            e = jnp.concatenate([E[ph, t, o] for o in range(YS)], axis=1)
            at = pl.ds(pl.multiple_of(t * CROWS, CROWS), CROWS)
            for h in range(2):
                Q[h] = Q[h] + jnp.dot(e, X[h, at], preferred_element_type=f32)

    def q_copy(ph):
        return rcopy(Q.at[1 - c], Qr.at[ph], q_s.at[ph], q_r.at[ph], sib)

    def ar_copy(ph, i):
        return rcopy(ar.at[ph, s], ar.at[ph, s], ar_s.at[ph, i], ar_r.at[ph, s], (samp_dev(i), f))

    def ar_recv(ph, i):
        o = samp_dev(i)
        return rcopy(ar.at[ph, o], ar.at[ph, o], ar_s.at[ph, i], ar_r.at[ph, o], (o, f))

    def fe_copy(ph, i):
        return rcopy(fe.at[ph, f], fe.at[ph, f], fe_s.at[ph, i], fe_r.at[ph, f], (s, feat_dev(i)))

    def fe_recv(ph, i):
        o = feat_dev(i)
        return rcopy(fe.at[ph, o], fe.at[ph, o], fe_s.at[ph, i], fe_r.at[ph, o], (s, o))

    def start_sums(ph):
        q_copy(ph).start()
        q_copy(ph).wait_recv()
        ar[ph, s] = pack(Q[c] + Qr[ph])
        for i in range(1, SAMP):
            ar_copy(ph, i).start()

    def finish_sums(ph):
        for i in range(1, SAMP):
            ar_recv(ph, i).wait_recv()
        total = ar[ph, 0]
        for o in range(1, SAMP):
            total = total + ar[ph, o]
        return total

    def drain(ph, grad):
        d_copy(ph).wait_send()
        q_copy(ph).wait_send()

        @pl.loop(0, CHUNKS)
        def _(t):
            for i in range(1, YS):
                rs_copy(ph, t, i, grad).wait_send()
                ag_copy(ph, t, i).wait_send()

    def exchange(ph, message):
        fe[ph, f] = message
        for i in range(1, FEAT):
            fe_copy(ph, i).start()
        for i in range(1, FEAT):
            fe_recv(ph, i).wait_recv()
        total = fe[ph, 0]
        for o in range(1, FEAT):
            total = total + fe[ph, o]
        return total

    d_recv(0).wait_recv()
    images(0, True)

    @pl.when(s < 10)
    def _():
        for i in range(1, FEAT):
            gf_recv(i).wait_recv()
        total = gparts[0]
        for o in range(1, FEAT):
            total = total + gparts[o]
        gall[s] = total
        for i in range(1, SAMP):
            gs_copy(i).start()

    pieces(0, True)
    collect(0)
    start_sums(0)

    sv = svals[...]
    low = jnp.min(jnp.min(sv, axis=1, keepdims=True), axis=0, keepdims=True)
    coef = (low + RIDGE) / (sv + RIDGE) - 1.0
    for jt in range(4):
        ccol[jt * 128 : (jt + 1) * 128, :] = column(coef[jt : jt + 1, :])
    V[...] = jnp.zeros_like(V)
    eye = jnp.where(rows_of(128) == lax.broadcasted_iota(jnp.int32, (128, 128), 1), 1.0, 0.0).astype(f32)

    @pl.loop(0, 4)
    def _(kb):
        off = lax.div(kb * (9 - kb), 2) - kb
        for l in range(4):
            src = lax.max(off + l, 0)

            @pl.when((l >= kb) & (src != s))
            def _():
                rcopy(gall.at[src], gall.at[src], gs_s.at[0], gs_r.at[src], (src, f)).wait_recv()

            @pl.when(l >= kb)
            def _():
                AK[:, l * 128 : (l + 1) * 128] = gall[src]

            @pl.when(l < kb)
            def _():
                AK[:, l * 128 : (l + 1) * 128] = jnp.zeros((128, 128), f32)

            AK[:, RANK + l * 128 : RANK + (l + 1) * 128] = jnp.where(kb == l, eye, 0.0)
        kcols = pl.ds(pl.multiple_of(kb * 128, 128), 128)

        @pl.when(kb > 0)
        def _():
            for l in range(4):
                lanes = slice(l * 256, (l + 1) * 256)
                AK[:, lanes] = AK[:, lanes] - lax.dot_general(
                    V[:, kcols], V[:, lanes], TN, precision=HI, preferred_element_type=f32
                )

        FA[...] = AK[:, kcols]
        FN[...] = eye
        factor_block(FA, FN)
        inv = FN[...]
        for l in range(8):
            lanes = slice(l * 128, (l + 1) * 128)
            blk = jnp.dot(inv, AK[:, lanes], precision=HI, preferred_element_type=f32)
            if l < 4:
                blk = jnp.where(l < kb, 0.0, blk)
            V[kcols, lanes] = blk

    def basis_dots(packed):
        rows = [lane_row(packed, lt // 2, lt % 2) for lt in range(LT)]

        @pl.loop(0, 8)
        def _(g):
            at = pl.ds(pl.multiple_of(g * 64, 64), 64)
            acc = BT[at, 0:128] * rows[0]
            for lt in range(1, LT):
                acc = acc + BT[at, lt * 128 : (lt + 1) * 128] * rows[lt]
            tmp[at, :] = acc

        return [jnp.sum(tmp[jt * 128 : (jt + 1) * 128, :].T, axis=0, keepdims=True) for jt in range(4)]

    def lanes_of(a, b):
        t = a * b
        t = jnp.sum(t[:, :128] + t[:, 128:256] + t[:, 256:], axis=0, keepdims=True)
        return t + pltpu.roll(t, 64, 1)

    lane = lax.broadcasted_iota(jnp.int32, (1, 128), 1)

    def both(x, z):
        return jnp.where(lane < 64, x, z)

    def halves(total):
        wide = lax.broadcasted_iota(jnp.int32, (8, 128), 1)
        lo = jnp.sum(jnp.where(wide < 64, total, 0.0), axis=1, keepdims=True)
        hi = jnp.sum(jnp.where(wide < 64, 0.0, total), axis=1, keepdims=True)
        return lo, hi

    def inner_part(p):
        y_rows = [jnp.zeros((8, 128), f32) for _ in range(4)]
        dot = jnp.zeros((8, 128), f32)
        for g in range(8):
            at = slice(g * 64, (g + 1) * 64)
            m = V[at, RANK : RANK + 128] * p[0]
            for l in range(1, 4):
                m = m + V[at, RANK + l * 128 : RANK + (l + 1) * 128] * p[l]
            inner = jnp.sum(m, axis=1, keepdims=True)
            ci = ccol[at, :] * inner
            d = ci * inner
            for b in range(8):
                dot = dot + d[b * 8 : (b + 1) * 8]
            for l in range(4):
                t = V[at, RANK + l * 128 : RANK + (l + 1) * 128] * ci
                for b in range(8):
                    y_rows[l] = y_rows[l] + t[b * 8 : (b + 1) * 8]
        return (
            [jnp.sum(t, axis=0, keepdims=True) for t in y_rows],
            jnp.sum(dot, axis=0, keepdims=True)[:, :1],
        )

    def basis_apply(y_rows):
        for jt in range(4):
            tmp[jt * 128 : (jt + 1) * 128, :] = column(y_rows[jt])

        def body(g, accs):
            out = list(accs)
            for b in range(4):
                at = pl.ds(pl.multiple_of(g * 32 + b * 8, 8), 8)
                col = tmp[at, :]
                for lt in range(LT):
                    out[lt] = out[lt] + BT[at, lt * 128 : (lt + 1) * 128] * col
            return tuple(out)

        accs = lax.fori_loop(0, 16, body, tuple(jnp.zeros((8, 128), f32) for _ in range(LT)))
        rows = [jnp.sum(t, axis=0, keepdims=True) for t in accs]
        tiles = [jnp.concatenate([rows[2 * k + h] for k in range(8)], axis=0) for h in range(2)]
        zero = jnp.zeros((1, 128), f32)
        last = jnp.concatenate([rows[16], rows[18], rows[17], rows[19]] + [zero] * 4, axis=0)
        return jnp.concatenate(tiles + [last], axis=1)

    def set_direction(ph, d):
        vec[1] = d
        dB[ph, c] = unpack(d).astype(bf16)
        d_copy(ph).start()

    NS = float(SAMP * ROWS)
    zrow = jnp.zeros((1, 128), f32)
    res = -(finish_sums(0) * (math.sqrt(F) / NS) + RIDGE * pack(w))
    drain(0, True)
    p0 = basis_dots(res)
    tot = exchange(0, jnp.concatenate(p0 + [zrow, zrow, both(lanes_of(res, res), zrow), zrow], axis=0))
    lo, hi = halves(tot)
    y_rows, py = inner_part([tot[i : i + 1] for i in range(4)])
    rr = lo[6:7]
    prow[...] = tot
    vec[0] = res
    vec[2] = jnp.zeros((8, 384), f32)
    scal[0:1, :] = jnp.broadcast_to(rr, (1, 128))
    scal[1:2, :] = jnp.broadcast_to(rr + py, (1, 128))
    set_direction(1, res + basis_apply(y_rows))

    @pl.loop(0, ITERS)
    def _(it):
        ph = it + 1
        d_recv(ph).wait_recv()
        images(ph, False)
        pieces(ph, False)
        collect(ph)
        start_sums(ph)
        drain(ph, False)
        d, r = vec[1], vec[0]
        q = finish_sums(ph) / NS + RIDGE * d
        bq = basis_dots(q)
        tot = exchange(ph, jnp.concatenate(bq + [
            both(lanes_of(d, q), lanes_of(r, d)),
            both(lanes_of(r, q), lanes_of(q, q)),
            both(lanes_of(r, r), zrow),
            zrow,
        ], axis=0))
        lo, hi = halves(tot)
        step = hi[4:5] / lo[4:5]
        x = vec[2] + step * d
        vec[2] = x

        @pl.when(it == ITERS - 1)
        def _():
            out[...] = unpack(x)

        @pl.when(it < ITERS - 1)
        def _():
            rn = r - step * q
            vec[0] = rn
            pn = prow[...] - step * tot
            prow[...] = pn
            y_rows, py = inner_part([pn[i : i + 1] for i in range(4)])
            rr = lo[6:7] - 2.0 * step * lo[5:6] + step * step * hi[5:6]
            new = rr + py
            beta = new / scal[1:2, 0:1]
            scal[1:2, :] = jnp.broadcast_to(new, (1, 128))
            set_direction(ph + 1, rn + basis_apply(y_rows) + beta * d)

    for t in range(CHUNKS):
        x_send(t).wait_send()

    @pl.when(s < 10)
    def _():
        for i in range(1, FEAT):
            gf_copy(i).wait_send()
        for i in range(1, SAMP):
            gs_copy(i).wait_send()

    @pl.loop(0, ITERS + 1)
    def _(ph):
        for i in range(1, SAMP):
            ar_copy(ph, i).wait_send()
        for i in range(1, FEAT):
            fe_copy(ph, i).wait_send()


def on_device(features, labels, weights, sketch_basis, sketch_values):
    vmem = pl.BlockSpec(memory_space=pltpu.VMEM)
    hbm = pl.BlockSpec(memory_space=pl.ANY)
    V = pltpu.VMEM
    dma = pltpu.SemaphoreType.DMA
    PH = ITERS + 1
    scratch = [
        V((2, HALF, COLS), bf16),
        V((K * COLS, RANK), f32),
        V((RANK, K * COLS), f32),
        V((PH, 2, 16, COLS), bf16),
        V((CHUNKS, YS, 16, PIECE), f32),
        V((CHUNKS, YS, 16, PIECE), bf16),
        V((CHUNKS, YS, 16, PIECE), f32),
        V((ITERS, CHUNKS, YS, 16, PIECE), bf16),
        V((CHUNKS, 16, PIECE), f32),
        V((PH, CHUNKS, YS, 16, PIECE), bf16),
        V((2, 16, COLS), f32),
        V((PH, 16, COLS), f32),
        V((PH, SAMP, 8, 384), f32),
        V((PH, FEAT, 8, 128), f32),
        V((FEAT, 128, 128), f32),
        V((SAMP, 128, 128), f32),
        V((RANK, 2 * RANK), f32),
        V((128, 2 * RANK), f32),
        V((128, 128), f32),
        V((128, 128), f32),
        V((RANK, 128), f32),
        V((RANK, 128), f32),
        V((3, 8, 384), f32),
        V((8, 128), f32),
        V((8, 128), f32),
        dma((CHUNKS,)), dma((CHUNKS,)), dma((CHUNKS,)), dma((K,)),
        dma((PH, CHUNKS, YS)), dma((PH, CHUNKS, YS)), dma((PH, CHUNKS, YS)), dma((PH, CHUNKS, YS)),
        dma((PH,)), dma((PH,)), dma((PH,)), dma((PH,)),
        dma((PH, SAMP)), dma((PH, SAMP)), dma((PH, FEAT)), dma((PH, FEAT)),
        dma((FEAT,)), dma((FEAT,)), dma((SAMP,)), dma((SAMP,)),
    ]
    step = pl.pallas_call(
        kernel,
        out_shape=jax.ShapeDtypeStruct((16, COLS), f32),
        in_specs=[hbm, vmem, vmem, hbm, vmem],
        out_specs=vmem,
        scratch_shapes=scratch,
        compiler_params=pltpu.CompilerParams(
            collective_id=0, has_side_effects=True, vmem_limit_bytes=60 * 1024 * 1024
        ),
        name="newton_step",
    )(
        features,
        labels.reshape(CORES * CHUNKS * YS, PIECE),
        jnp.pad(weights, ((0, 6), (0, 0))),
        sketch_basis.reshape(K * COLS, RANK),
        sketch_values.reshape(4, 128),
    )
    return step[:K]


def solution(mesh):
    in_specs = (P("samp", "feat"), P("samp"), P(None, "feat"), P(None, "feat", None), P())
    return jax.shard_map(
        on_device, mesh=mesh, in_specs=in_specs, out_specs=P(None, "feat"), check_vma=False
    )
```

time: 576 us -> 141 us (0.24); the launches traced: 570 us -> 141 us
  blocking collectives: 251 us -> 0 us
  Pallas kernels: 0 us -> 137 us
  other arithmetic: 129 us -> 0 us
  matrix products: 93.6 us -> 0 us
  starting transfers between devices: 27.4 us -> 0 us
  local copies, waits for them, and re-layouts: 30.1 us -> 4.12 us
  between operations: 23.9 us -> 0.01 us
  waiting for transfers between devices: 15.4 us -> 0 us
    pallas_call x0 -> x1, Pallas kernels: none -> 137 us  [on_device(): pl.pallas_call(kernel, out_shape=jax.ShapeDtypeStruct((16, COLS), f32), i...]
    all_gather x4 -> x0, blocking collectives: 137 us -> none  [the longest x1 96.5 us: on_device(): weights_b = lax.all_gather(weights_b, 'feat', axis=1, tiled=True)]
    another operation x21 -> x0, other arithmetic: 119 us -> none  [the longest x14 79 us: on_device(): factor = jnp.linalg.cholesky(gram_matrix)]
    all_to_all x13 -> x0, blocking collectives: 114 us -> none  [the longest x10 89.3 us: copy_for_each(): lax.all_to_all(jnp.broadcast_to(shard[None], (devices, *shard.shape)), ax...]
    dot_general x15 -> x0, matrix products: 83.1 us -> none  [the longest x3 20.5 us: precondition(): jnp.dot(basis_own, outer_coords, precision=lax.Precision.HIGHEST)]
    all_to_all x5 -> x0, starting transfers between devices: 27.4 us -> none  [the longest x3 17.5 us: copy_for_each(): lax.all_to_all(jnp.broadcast_to(shard[None], (devices, *shard.shape)), ax...]
    all_to_all x5 -> x0, waiting for transfers between devices: 15.3 us -> none  [the longest x3 11.4 us: copy_for_each(): lax.all_to_all(jnp.broadcast_to(shard[None], (devices, *shard.shape)), ax...]
    all_to_all x1 -> x0, local copies, waits for them, and re-layouts: 11.6 us -> none  [on_device(): lax.all_to_all(features, 'feat', split_axis=0, concat_axis=1, tiled=True)]
  transfers between devices with their start and end apart: 6 -> 0, of which waited for: 3 -> 0; matrix products, arithmetic and copies ran while one was open for 26% -> 0% of each run, Pallas kernels for 0% -> 0%
where the time goes in v1:
time: 141 us
  Pallas kernels  137 us (97%)
  local copies, waits for them, and re-layouts  4.12 us (3%)
    pallas_call x1, Pallas kernels, on_device(): pl.pallas_call(kernel, out_shape=jax.ShapeDtypeStruct((16, COLS), f32), i...  137 us

profile of v1, /device:TPU:1, one launch (start us, length us, event | category | flops | bytes accessed | tf_op | source)
XLA Modules:
  0.0 140.9 jit_solution(3667072762998537888)
XLA Ops:
  0.0 1.3 pad.4.w16
  1.3 1.5 %reshape.9.labels = s32[32,512]{1,0:T(8,128)} reshape(s32[16384]{0:T(1024)} %param.6) | data formatting | bytes 131072 | tf_op jit(solution)/shard_map/reshape | solution.py:592
  2.8 136.8 %newton_step.1 = f32[16,256]{1,0:T(8,128)} custom-call(bf16[16384,256]{1,0:T(8,128)(2,1)} %feat.1, s32[32,512]{1,0:T(8,128)} %reshape.9.labels, f32[16,256]{1,0:T(8,128)} %pad.4.w16, f32[2560,512]{1,0:T(8,128)} %bitcast.3, f32[4,128]{1,0:T(4,128)} %bitcast.5), custom_call_target="tpu_custom_call" | custom-call | tf_op jit(solution)/shard_map/newton_step/pallas_call | solution.py:580
  139.6 1.3 copy.7

commit v2 on v1

--- a/solution.py
+++ b/solution.py
@@ -26,6 +26,19 @@
 HI = lax.Precision.HIGHEST
 NT = (((1,), (1,)), ((), ()))
 TN = (((0,), (0,)), ((), ()))
+OFFS = (0, 4, 7, 9)
+FAR_SAMP = sorted(range(1, SAMP), key=lambda i: -(min(i // 4, 4 - i // 4) + min(i % 4, 4 - i % 4)))
+FAR_FEAT = (4, 5, 3, 2, 6, 7, 1)
+
+
+def scoped(name):
+    def wrap(fn):
+        @functools.wraps(fn)
+        def run(*args):
+            with jax.named_scope(name):
+                return fn(*args)
+        return run
+    return wrap
 
 
 def rcopy(src, dst, send, recv, dev):
@@ -64,42 +77,62 @@
     return jnp.broadcast_to(row, (128, 128)).T
 
 
+def lane_bcast(x, j):
+    return jnp.broadcast_to(x[:, j : j + 1], (x.shape[0], 128))
+
+
+@scoped('factor')
 def factor_block(A, N):
+    diag = [lane_bcast(A[0:8, :], j) for j in range(8)]
     for p in range(16):
         lo = 8 * p
-        n = 128 - lo
-        ap = A[lo:128, :]
-        cols = [jnp.broadcast_to(ap[:, lo + j : lo + j + 1], (n, 128)) for j in range(8)]
+        more = lo + 8 < 128
+        if more:
+            below = [lane_bcast(A[lo + 8 : 128, :], lo + j) for j in range(8)]
+            ahead = [lane_bcast(A[lo + 8 : lo + 16, :], lo + 8 + j) for j in range(8)]
+        rs, cs = [], []
+        for j in range(8):
+            r = lax.rsqrt(diag[j][j : j + 1, :])
+            c = diag[j] * r
+            for k in range(j + 1, 8):
+                diag[k] = diag[k] - c * c[k : k + 1, :]
+            rs.append(r)
+            cs.append(c)
         arow, nrow = A[lo : lo + 8, :], N[lo : lo + 8, :]
-        cs, us, ns = [], [], []
+        us, ns = [], []
         for j in range(8):
-            r = lax.rsqrt(cols[j][j : j + 1, :])
-            c = cols[j] * r
-            u = arow[j : j + 1, :] * r
-            v = nrow[j : j + 1, :] * r
-            for k in range(j + 1, 8):
-                cols[k] = cols[k] - c * c[k : k + 1, :]
-            arow = arow - c[:8] * u
-            nrow = nrow - c[:8] * v
-            cs.append(c)
-            us.append(u)
-            ns.append(v)
-        if n > 8:
-            at, nt = A[lo + 8 : 128, :], N[lo + 8 : 128, :]
+            us.append(arow[j : j + 1, :] * rs[j])
+            ns.append(nrow[j : j + 1, :] * rs[j])
+            if j < 7:
+                arow = arow - cs[j] * us[j]
+                nrow = nrow - cs[j] * ns[j]
+        N[lo : lo + 8, :] = jnp.concatenate(ns, axis=0)
+        if not more:
+            continue
+        bs = []
+        for j in range(8):
+            t = below[j]
+            for i in range(j):
+                t = t - bs[i] * cs[i][j : j + 1, :]
+            bs.append(t * rs[j])
+        for k in range(8):
             for j in range(8):
-                at = at - cs[j][8:] * us[j]
-                nt = nt - cs[j][8:] * ns[j]
-            A[lo + 8 : 128, :] = at
-            N[lo + 8 : 128, :] = nt
-        N[lo : lo + 8, :] = jnp.concatenate(ns, axis=0)
+                ahead[k] = ahead[k] - bs[j][:8] * bs[j][k : k + 1, :]
+        diag = ahead
+        at, nt = A[lo + 8 : 128, :], N[lo + 8 : 128, :]
+        for j in range(8):
+            at = at - bs[j] * us[j]
+            nt = nt - bs[j] * ns[j]
+        A[lo + 8 : 128, :] = at
+        N[lo + 8 : 128, :] = nt
 
 
 def kernel(
-    feat, labels, w16, basis, svals, out,
+    feat, labels, weights, basis, svals, out,
     X, bst, BT, dB, imgf, imgb, recvg, recvh, prob, E, Q, Qr, ar, fe,
-    gparts, gall, V, AK, FA, FN, ccol, tmp, vec, prow, scal,
+    lab, gpart, grecv, gall, V, acc, FA, FN, ccol, tmp, vec, prow, scal,
     sx_own, sx_s, sx_r, s_b, rs_s, rs_r, ag_s, ag_r, q_s, q_r, d_s, d_r,
-    ar_s, ar_r, fe_s, fe_r, gf_s, gf_r, gs_s, gs_r,
+    ar_s, ar_r, fe_s, fe_r, gf_s, gf_r, gs_s, gs_r, gy_s, gy_r, l_s,
 ):
     s = lax.axis_index("samp")
     f = lax.axis_index("feat")
@@ -135,8 +168,13 @@
         dst = X.at[1 - c, pl.ds(t * CROWS, CROWS)]
         return rcopy(dst, dst, sx_s.at[t], sx_r.at[t], sib)
 
+    def lab_copy(t):
+        start = pl.multiple_of(c * HALF + t * CROWS + y * PIECE, PIECE)
+        return pltpu.make_async_copy(labels.at[pl.ds(start, PIECE)], lab.at[t, 0], l_s.at[t])
+
     for t in range(CHUNKS):
         x_own(t).start()
+        lab_copy(t).start()
 
     def d_copy(ph):
         return rcopy(dB.at[ph, c], dB.at[ph, c], d_s.at[ph], d_r.at[ph], sib)
@@ -150,14 +188,11 @@
     for i in range(1, SAMP):
         pl.semaphore_signal(barrier, inc=1, device_id=(samp_dev(i), f), device_id_type=pl.DeviceIdType.MESH)
 
-    w = w16[...]
+    w = jnp.concatenate([weights[...], jnp.zeros((16 - K, COLS), f32)], axis=0)
     dB[0, c] = w.astype(bf16)
-    pl.semaphore_wait(barrier, FEAT - 1 + SAMP - 1)
-    d_copy(0).start()
-    for t in range(CHUNKS):
-        x_send(t).start()
 
     @pl.loop(0, K)
+    @scoped('transpose')
     def _(k):
         pltpu.make_async_copy(
             basis.at[pl.ds(k * COLS, COLS)], bst.at[pl.ds(k * COLS, COLS)], s_b.at[k]
@@ -171,30 +206,61 @@
     ba = sum((blk_id >= e).astype(jnp.int32) for e in (4, 7, 9))
     bb = blk_id - lax.div(ba * (9 - ba), 2) + ba
 
-    def gram_step(kk, acc):
-        cols = pl.ds(pl.multiple_of(kk * 256, 256), 256)
-        return acc + lax.dot_general(
-            BT[pl.ds(pl.multiple_of(ba * 128, 128), 128), cols],
-            BT[pl.ds(pl.multiple_of(bb * 128, 128), 128), cols],
+    with jax.named_scope('gram'):
+        block = lax.dot_general(
+            BT[pl.ds(pl.multiple_of(ba * 128, 128), 128), :],
+            BT[pl.ds(pl.multiple_of(bb * 128, 128), 128), :],
             NT, precision=HI, preferred_element_type=f32,
         )
-
-    gparts[f] = lax.fori_loop(0, K, gram_step, jnp.zeros((128, 128), f32))
+        for g in range(FEAT):
+            gpart[g] = block[g * 16 : (g + 1) * 16]
 
     def gf_copy(i):
-        return rcopy(gparts.at[f], gparts.at[f], gf_s.at[i], gf_r.at[f], (s, feat_dev(i)))
+        o = feat_dev(i)
+        return rcopy(gpart.at[o], grecv.at[f], gf_s.at[i], gf_r.at[f], (s, o))
 
     def gf_recv(i):
-        src = feat_dev(i)
-        return rcopy(gparts.at[src], gparts.at[src], gf_s.at[i], gf_r.at[src], (s, src))
+        o = feat_dev(i)
+        return rcopy(grecv.at[o], grecv.at[o], gf_s.at[i], gf_r.at[o], (s, o))
 
     def gs_copy(i):
-        return rcopy(gall.at[s], gall.at[s], gs_s.at[i], gs_r.at[s], (samp_dev(i), f))
+        return rcopy(gall.at[f, s], gall.at[f, s], gs_s.at[i], gs_r.at[s], (samp_dev(i), f))
+
+    def gs_recv(o):
+        return rcopy(gall.at[f, o], gall.at[f, o], gs_s.at[0], gs_r.at[o], (o, f))
+
+    def gy_copy(kb, i):
+        at = pl.ds(OFFS[kb], 4 - kb)
+        return rcopy(gall.at[f, at], gall.at[f, at], gy_s.at[kb, i], gy_r.at[kb, f], (s, feat_dev(i)))
+
+    def gy_recv(kb, i):
+        at, o = pl.ds(OFFS[kb], 4 - kb), feat_dev(i)
+        return rcopy(gall.at[o, at], gall.at[o, at], gy_s.at[kb, i], gy_r.at[kb, o], (s, o))
+
+    with jax.named_scope('barrier'):
+        pl.semaphore_wait(barrier, FEAT - 1 + SAMP - 1)
 
     @pl.when(s < 10)
     def _():
+        for i in FAR_FEAT:
+            gf_copy(i).start()
+
+    d_copy(0).start()
+    for t in range(CHUNKS):
+        x_send(t).start()
+
+    @pl.when(s < 10)
+    @scoped('gram_sum')
+    def _():
         for i in range(1, FEAT):
-            gf_copy(i).start()
+            gf_recv(i).wait_recv()
+        grecv[f] = gpart[f]
+        total = grecv[0]
+        for o in range(1, FEAT):
+            total = total + grecv[o]
+        gall[f, s] = total
+        for i in FAR_SAMP:
+            gs_copy(i).start()
 
     def rs_copy(ph, t, i, grad):
         o = y_dev(i)
@@ -214,6 +280,7 @@
         o = y_dev(i)
         return rcopy(E.at[ph, t, o], E.at[ph, t, o], ag_s.at[ph, t, i], ag_r.at[ph, t, o], (s, CORES * o + c))
 
+    @scoped('images')
     def images(ph, grad):
         @pl.loop(0, CHUNKS)
         def _(t):
@@ -231,6 +298,7 @@
             for i in range(1, YS):
                 rs_copy(ph, t, i, grad).start()
 
+    @scoped('pieces')
     def pieces(ph, grad):
         @pl.loop(0, CHUNKS)
         def _(t):
@@ -248,7 +316,8 @@
                 ex = jnp.exp(logits - top)
                 pr = ex / jnp.sum(ex, axis=0, keepdims=True)
                 prob[t] = pr
-                own = labels[pl.ds(c * (CHUNKS * YS) + t * YS + y, 1), :]
+                lab_copy(t).wait()
+                own = lab[t]
                 coeffs = pr - jnp.where(row == own, 1.0, 0.0)
             else:
                 pr = prob[t]
@@ -258,6 +327,7 @@
             for i in range(1, YS):
                 ag_copy(ph, t, i).start()
 
+    @scoped('collect')
     def collect(ph):
         Q[...] = jnp.zeros_like(Q)
 
@@ -287,13 +357,15 @@
         o = feat_dev(i)
         return rcopy(fe.at[ph, o], fe.at[ph, o], fe_s.at[ph, i], fe_r.at[ph, o], (s, o))
 
+    @scoped('sums_start')
     def start_sums(ph):
         q_copy(ph).start()
         q_copy(ph).wait_recv()
         ar[ph, s] = pack(Q[c] + Qr[ph])
-        for i in range(1, SAMP):
+        for i in FAR_SAMP:
             ar_copy(ph, i).start()
 
+    @scoped('sums_finish')
     def finish_sums(ph):
         for i in range(1, SAMP):
             ar_recv(ph, i).wait_recv()
@@ -302,6 +374,7 @@
             total = total + ar[ph, o]
         return total
 
+    @scoped('drain')
     def drain(ph, grad):
         d_copy(ph).wait_send()
         q_copy(ph).wait_send()
@@ -312,9 +385,10 @@
                 rs_copy(ph, t, i, grad).wait_send()
                 ag_copy(ph, t, i).wait_send()
 
+    @scoped('exchange')
     def exchange(ph, message):
         fe[ph, f] = message
-        for i in range(1, FEAT):
+        for i in FAR_FEAT:
             fe_copy(ph, i).start()
         for i in range(1, FEAT):
             fe_recv(ph, i).wait_recv()
@@ -323,72 +397,80 @@
             total = total + fe[ph, o]
         return total
 
-    d_recv(0).wait_recv()
+    with jax.named_scope('dwait'):
+        d_recv(0).wait_recv()
     images(0, True)
 
-    @pl.when(s < 10)
-    def _():
-        for i in range(1, FEAT):
-            gf_recv(i).wait_recv()
-        total = gparts[0]
-        for o in range(1, FEAT):
-            total = total + gparts[o]
-        gall[s] = total
-        for i in range(1, SAMP):
-            gs_copy(i).start()
-
+    @scoped('gram_gather')
+    def gram_gather():
+        for kb in range(4):
+            for o in range(OFFS[kb], OFFS[kb] + 4 - kb):
+                @pl.when(s != o)
+                def _():
+                    gs_recv(o).wait_recv()
+            for i in FAR_FEAT:
+                gy_copy(kb, i).start()
+
+    gram_gather()
     pieces(0, True)
-    collect(0)
-    start_sums(0)
 
     sv = svals[...]
     low = jnp.min(jnp.min(sv, axis=1, keepdims=True), axis=0, keepdims=True)
     coef = (low + RIDGE) / (sv + RIDGE) - 1.0
     for jt in range(4):
         ccol[jt * 128 : (jt + 1) * 128, :] = column(coef[jt : jt + 1, :])
-    V[...] = jnp.zeros_like(V)
     eye = jnp.where(rows_of(128) == lax.broadcasted_iota(jnp.int32, (128, 128), 1), 1.0, 0.0).astype(f32)
 
-    @pl.loop(0, 4)
-    def _(kb):
-        off = lax.div(kb * (9 - kb), 2) - kb
-        for l in range(4):
-            src = lax.max(off + l, 0)
-
-            @pl.when((l >= kb) & (src != s))
-            def _():
-                rcopy(gall.at[src], gall.at[src], gs_s.at[0], gs_r.at[src], (src, f)).wait_recv()
-
-            @pl.when(l >= kb)
-            def _():
-                AK[:, l * 128 : (l + 1) * 128] = gall[src]
-
-            @pl.when(l < kb)
-            def _():
-                AK[:, l * 128 : (l + 1) * 128] = jnp.zeros((128, 128), f32)
-
-            AK[:, RANK + l * 128 : RANK + (l + 1) * 128] = jnp.where(kb == l, eye, 0.0)
-        kcols = pl.ds(pl.multiple_of(kb * 128, 128), 128)
-
-        @pl.when(kb > 0)
-        def _():
-            for l in range(4):
-                lanes = slice(l * 256, (l + 1) * 256)
-                AK[:, lanes] = AK[:, lanes] - lax.dot_general(
-                    V[:, kcols], V[:, lanes], TN, precision=HI, preferred_element_type=f32
-                )
-
-        FA[...] = AK[:, kcols]
-        FN[...] = eye
-        factor_block(FA, FN)
-        inv = FN[...]
-        for l in range(8):
-            lanes = slice(l * 128, (l + 1) * 128)
-            blk = jnp.dot(inv, AK[:, lanes], precision=HI, preferred_element_type=f32)
-            if l < 4:
-                blk = jnp.where(l < kb, 0.0, blk)
-            V[kcols, lanes] = blk
-
+    def lanes(a, b):
+        return slice(a * 128, b * 128)
+
+    def dot_hi(a, b, dims=(((1,), (0,)), ((), ()))):
+        return lax.dot_general(a, b, dims, precision=HI, preferred_element_type=f32)
+
+    def gram_block(k, l):
+        blk = jnp.concatenate([gall[o, OFFS[k] + l - k] for o in range(FEAT)], axis=0)
+        return blk if k == 0 else blk - acc[k, :, lanes(l, l + 1)]
+
+    def add_to(k, i, a, b):
+        term = dot_hi(V[k, :, lanes(i, i + 1)], V[k, :, lanes(a, b)], TN)
+        first = k == 0 if b <= 4 else k == a - 4
+        acc[i, :, lanes(a, b)] = term if first else acc[i, :, lanes(a, b)] + term
+
+    def rest_of(k):
+        inv = V[k, :, lanes(4 + k, 5 + k)]
+        if k < 2:
+            V[k, :, lanes(k + 2, 4)] = dot_hi(inv, jnp.concatenate([gram_block(k, l) for l in range(k + 2, 4)], axis=1))
+        if k > 0:
+            V[k, :, lanes(4, 4 + k)] = -dot_hi(inv, acc[k, :, lanes(4, 4 + k)])
+        for i in range(k + 1, 4):
+            if i > k + 1:
+                add_to(k, i, i, 4)
+            elif i < 3:
+                add_to(k, i, i + 1, 4)
+            if k > 0:
+                add_to(k, i, 4, 4 + k)
+            add_to(k, i, 4 + k, 5 + k)
+
+    for kb in range(4):
+        with jax.named_scope('chol_wait'):
+            for i in range(1, FEAT):
+                gy_recv(kb, i).wait_recv()
+        with jax.named_scope('chol'):
+            FA[...] = gram_block(kb, kb)
+            FN[...] = eye
+            if kb > 0:
+                rest_of(kb - 1)
+            factor_block(FA, FN)
+            V[kb, :, lanes(4 + kb, 5 + kb)] = FN[...]
+            if kb < 3:
+                V[kb, :, lanes(kb + 1, kb + 2)] = dot_hi(FN[...], gram_block(kb, kb + 1))
+                add_to(kb, kb + 1, kb + 1, kb + 2)
+        if kb == 1:
+            collect(0)
+            start_sums(0)
+    rest_of(3)
+
+    @scoped('basis_dots')
     def basis_dots(packed):
         rows = [lane_row(packed, lt // 2, lt % 2) for lt in range(LT)]
 
@@ -418,21 +500,22 @@
         hi = jnp.sum(jnp.where(wide < 64, 0.0, total), axis=1, keepdims=True)
         return lo, hi
 
+    @scoped('inner')
     def inner_part(p):
         y_rows = [jnp.zeros((8, 128), f32) for _ in range(4)]
         dot = jnp.zeros((8, 128), f32)
         for g in range(8):
-            at = slice(g * 64, (g + 1) * 64)
-            m = V[at, RANK : RANK + 128] * p[0]
-            for l in range(1, 4):
-                m = m + V[at, RANK + l * 128 : RANK + (l + 1) * 128] * p[l]
+            kb, at, crow = g // 2, slice((g % 2) * 64, (g % 2) * 64 + 64), slice(g * 64, (g + 1) * 64)
+            m = V[kb, at, lanes(4, 5)] * p[0]
+            for l in range(1, kb + 1):
+                m = m + V[kb, at, lanes(4 + l, 5 + l)] * p[l]
             inner = jnp.sum(m, axis=1, keepdims=True)
-            ci = ccol[at, :] * inner
+            ci = ccol[crow, :] * inner
             d = ci * inner
             for b in range(8):
                 dot = dot + d[b * 8 : (b + 1) * 8]
-            for l in range(4):
-                t = V[at, RANK + l * 128 : RANK + (l + 1) * 128] * ci
+            for l in range(kb + 1):
+                t = V[kb, at, lanes(4 + l, 5 + l)] * ci
                 for b in range(8):
                     y_rows[l] = y_rows[l] + t[b * 8 : (b + 1) * 8]
         return (
@@ -440,6 +523,7 @@
             jnp.sum(dot, axis=0, keepdims=True)[:, :1],
         )
 
+    @scoped('basis_apply')
     def basis_apply(y_rows):
         for jt in range(4):
             tmp[jt * 128 : (jt + 1) * 128, :] = column(y_rows[jt])
@@ -484,7 +568,8 @@
     @pl.loop(0, ITERS)
     def _(it):
         ph = it + 1
-        d_recv(ph).wait_recv()
+        with jax.named_scope('dwait'):
+            d_recv(ph).wait_recv()
         images(ph, False)
         pieces(ph, False)
         collect(ph)
@@ -506,7 +591,7 @@
 
         @pl.when(it == ITERS - 1)
         def _():
-            out[...] = unpack(x)
+            out[...] = unpack(x)[:K]
 
         @pl.when(it < ITERS - 1)
         def _():
@@ -530,6 +615,10 @@
             gf_copy(i).wait_send()
         for i in range(1, SAMP):
             gs_copy(i).wait_send()
+
+    for kb in range(4):
+        for i in range(1, FEAT):
+            gy_copy(kb, i).wait_send()
 
     @pl.loop(0, ITERS + 1)
     def _(ph):
@@ -560,10 +649,12 @@
         V((PH, 16, COLS), f32),
         V((PH, SAMP, 8, 384), f32),
         V((PH, FEAT, 8, 128), f32),
-        V((FEAT, 128, 128), f32),
-        V((SAMP, 128, 128), f32),
-        V((RANK, 2 * RANK), f32),
-        V((128, 2 * RANK), f32),
+        V((CHUNKS, 1, PIECE), jnp.int32),
+        V((FEAT, 16, 128), f32),
+        V((FEAT, 16, 128), f32),
+        V((FEAT, SAMP, 16, 128), f32),
+        V((4, 128, 2 * RANK), f32),
+        V((4, 128, 2 * RANK), f32),
         V((128, 128), f32),
         V((128, 128), f32),
         V((RANK, 128), f32),
@@ -576,11 +667,12 @@
         dma((PH,)), dma((PH,)), dma((PH,)), dma((PH,)),
         dma((PH, SAMP)), dma((PH, SAMP)), dma((PH, FEAT)), dma((PH, FEAT)),
         dma((FEAT,)), dma((FEAT,)), dma((SAMP,)), dma((SAMP,)),
+        dma((4, FEAT)), dma((4, FEAT)), dma((CHUNKS,)),
     ]
     step = pl.pallas_call(
         kernel,
-        out_shape=jax.ShapeDtypeStruct((16, COLS), f32),
-        in_specs=[hbm, vmem, vmem, hbm, vmem],
+        out_shape=jax.ShapeDtypeStruct((K, COLS), f32),
+        in_specs=[hbm, hbm, vmem, hbm, vmem],
         out_specs=vmem,
         scratch_shapes=scratch,
         compiler_params=pltpu.CompilerParams(
@@ -589,12 +681,12 @@
         name="newton_step",
     )(
         features,
-        labels.reshape(CORES * CHUNKS * YS, PIECE),
-        jnp.pad(weights, ((0, 6), (0, 0))),
+        labels,
+        weights,
         sketch_basis.reshape(K * COLS, RANK),
         sketch_values.reshape(4, 128),
     )
-    return step[:K]
+    return step
 
 
 def solution(mesh):

time: 141 us -> 122 us (0.87)
  Pallas kernels: 137 us -> 121 us
  local copies, waits for them, and re-layouts: 4.12 us -> 1.32 us
    pallas_call x1, Pallas kernels: 137 us -> 121 us  [on_device(): pl.pallas_call(kernel, out_shape=jax.ShapeDtypeStruct((K, COLS), f32), in...]
    reshape x1 -> x0, local copies, waits for them, and re-layouts: 1.47 us -> none  [on_device(): labels.reshape(CORES * CHUNKS * YS, PIECE)]
where the time goes in v2:
time: 122 us
  Pallas kernels  121 us (99%)
  local copies, waits for them, and re-layouts  1.32 us (1%)
    pallas_call x1, Pallas kernels, on_device(): pl.pallas_call(kernel, out_shape=jax.ShapeDtypeStruct((K, COLS), f32), in...  121 us

profile of v2, /device:TPU:1, one launch (start us, length us, event | category | flops | bytes accessed | tf_op | source)
XLA Modules:
  0.0 122.1 jit_solution(448893312301107696)
XLA Ops:
  0.0 120.8 %newton_step.1 = f32[10,256]{1,0:T(8,128)} custom-call(bf16[16384,256]{1,0:T(8,128)(2,1)} %feat.1, s32[16384]{0:T(1024)} %labels.1, f32[10,256]{1,0:T(8,128)} %weights.1, f32[2560,512]{1,0:T(8,128)} %bitcast.2, f32[4,128]{1,0:T(4,128)} %bitcast.3), custom_call_target="tpu_custom_call" | custom-call | tf_op jit(solution)/shard_map/newton_step/pallas_call | solution.py:672
  120.8 1.3 %copy.7 = f32[10,256]{1,0:T(8,128)} copy(f32[10,256]{1,0:T(8,128)} %newton_step.1) | data formatting | bytes 20480

commit v3 on v2

--- a/solution.py
+++ b/solution.py
@@ -18,6 +18,7 @@
 CHUNKS = 4
 CROWS = HALF // CHUNKS
 PIECE = CROWS // YS
+PWIDE = PIECE + 128
 COLS = 256
 K = 10
 RANK = 512
@@ -27,6 +28,7 @@
 NT = (((1,), (1,)), ((), ()))
 TN = (((0,), (0,)), ((), ()))
 OFFS = (0, 4, 7, 9)
+MSGS = ((0, 1), (1, 3), (4, 3), (7, 2), (9, 1))
 FAR_SAMP = sorted(range(1, SAMP), key=lambda i: -(min(i // 4, 4 - i // 4) + min(i % 4, 4 - i % 4)))
 FAR_FEAT = (4, 5, 3, 2, 6, 7, 1)
 
@@ -64,6 +66,38 @@
     left = jnp.where(row < 2, third, 0.0)
     right = jnp.where(row < 2, pltpu.roll(third, 6, 0), 0.0)
     return jnp.concatenate([packed[:, :256], jnp.concatenate([left, right], axis=1)], axis=0)
+
+
+def pack_piece(wide):
+    low = wide[8:16]
+    last = low[:, :128]
+    for q in range(1, PIECE // 128):
+        last = last + pltpu.roll(low[:, q * 128 : (q + 1) * 128], 2 * q, 0)
+    return jnp.concatenate([wide[:8], last], axis=1)
+
+
+def unpack_piece(packed):
+    last = packed[:, PIECE:]
+    row = rows_of(8)
+    low = [
+        jnp.where(row < 2, pltpu.roll(last, (8 - 2 * q) % 8, 0) if q else last, 0.0) for q in range(PIECE // 128)
+    ]
+    return jnp.concatenate([packed[:, :PIECE], jnp.concatenate(low, axis=1)], axis=0)
+
+
+def spread_piece(packed):
+    last = packed[:, PIECE:]
+    row = rows_of(8)
+    low = [jnp.where((row >= 2 * q) & (row < 2 * q + 2), last, 0.0) for q in range(PIECE // 128)]
+    return jnp.concatenate([packed[:, :PIECE], jnp.concatenate(low, axis=1)], axis=0)
+
+
+def fold_rows(wide):
+    low = wide[8:16]
+    low = low + pltpu.roll(low, 4, 0)
+    low = low + pltpu.roll(low, 2, 0)
+    row = lax.broadcasted_iota(jnp.int32, low.shape, 0)
+    return jnp.concatenate([wide[:8], jnp.where(row < 2, low, 0.0)], axis=0)
 
 
 def lane_row(packed, k, h):
@@ -129,7 +163,7 @@
 
 def kernel(
     feat, labels, weights, basis, svals, out,
-    X, bst, BT, dB, imgf, imgb, recvg, recvh, prob, E, Q, Qr, ar, fe,
+    X, bst, BT, dB, imgf, imgb, recvg, recvh, prob, E, Q, Qr, ar, dots, fe,
     lab, gpart, grecv, gall, V, acc, FA, FN, ccol, tmp, vec, prow, scal,
     sx_own, sx_s, sx_r, s_b, rs_s, rs_r, ag_s, ag_r, q_s, q_r, d_s, d_r,
     ar_s, ar_r, fe_s, fe_r, gf_s, gf_r, gs_s, gs_r, gy_s, gy_r, l_s,
@@ -172,9 +206,6 @@
         start = pl.multiple_of(c * HALF + t * CROWS + y * PIECE, PIECE)
         return pltpu.make_async_copy(labels.at[pl.ds(start, PIECE)], lab.at[t, 0], l_s.at[t])
 
-    for t in range(CHUNKS):
-        x_own(t).start()
-        lab_copy(t).start()
 
     def d_copy(ph):
         return rcopy(dB.at[ph, c], dB.at[ph, c], d_s.at[ph], d_r.at[ph], sib)
@@ -202,6 +233,10 @@
                 blk = bst[pl.ds(pl.multiple_of(k * COLS + h * 128, 128), 128), jt * 128 : (jt + 1) * 128]
                 BT[jt * 128 : (jt + 1) * 128, pl.ds(pl.multiple_of(k * COLS + h * 128, 128), 128)] = blk.T
 
+    for t in range(CHUNKS):
+        x_own(t).start()
+        lab_copy(t).start()
+
     blk_id = lax.min(s, 9)
     ba = sum((blk_id >= e).astype(jnp.int32) for e in (4, 7, 9))
     bb = blk_id - lax.div(ba * (9 - ba), 2) + ba
@@ -229,13 +264,13 @@
     def gs_recv(o):
         return rcopy(gall.at[f, o], gall.at[f, o], gs_s.at[0], gs_r.at[o], (o, f))
 
-    def gy_copy(kb, i):
-        at = pl.ds(OFFS[kb], 4 - kb)
-        return rcopy(gall.at[f, at], gall.at[f, at], gy_s.at[kb, i], gy_r.at[kb, f], (s, feat_dev(i)))
-
-    def gy_recv(kb, i):
-        at, o = pl.ds(OFFS[kb], 4 - kb), feat_dev(i)
-        return rcopy(gall.at[o, at], gall.at[o, at], gy_s.at[kb, i], gy_r.at[kb, o], (s, o))
+    def gy_copy(m, i):
+        at = pl.ds(*MSGS[m])
+        return rcopy(gall.at[f, at], gall.at[f, at], gy_s.at[m, i], gy_r.at[m, f], (s, feat_dev(i)))
+
+    def gy_recv(m, i):
+        at, o = pl.ds(*MSGS[m]), feat_dev(i)
+        return rcopy(gall.at[o, at], gall.at[o, at], gy_s.at[m, i], gy_r.at[m, o], (s, o))
 
     with jax.named_scope('barrier'):
         pl.semaphore_wait(barrier, FEAT - 1 + SAMP - 1)
@@ -284,14 +319,20 @@
     def images(ph, grad):
         @pl.loop(0, CHUNKS)
         def _(t):
+            at = pl.ds(pl.multiple_of(t * CROWS, CROWS), CROWS)
             if grad:
                 x_own(t).wait()
+            img = lax.dot_general(dB[ph, c], X[c, at], NT, preferred_element_type=f32)
+
+            @pl.when(t == 0)
+            def _():
+                d_recv(ph).wait_recv()
+
+            if grad:
                 x_recv(t).wait_recv()
-            at = pl.ds(pl.multiple_of(t * CROWS, CROWS), CROWS)
-            img = lax.dot_general(dB[ph, 0], X[0, at], NT, preferred_element_type=f32)
-            img = img + lax.dot_general(dB[ph, 1], X[1, at], NT, preferred_element_type=f32)
+            img = img + lax.dot_general(dB[ph, 1 - c], X[1 - c, at], NT, preferred_element_type=f32)
             for o in range(YS):
-                piece = img[:, o * PIECE : (o + 1) * PIECE]
+                piece = pack_piece(img[:, o * PIECE : (o + 1) * PIECE])
                 imgf[t, o] = piece
                 if not grad:
                     imgb[t, o] = piece.astype(bf16)
@@ -308,6 +349,7 @@
             for i in range(1, YS):
                 o = y_dev(i)
                 total = total + (recvg[t, o] if grad else recvh[ph - 1, t, o].astype(f32))
+            total = unpack_piece(total)
             if grad:
                 logits = total / math.sqrt(F)
                 row = lax.broadcasted_iota(jnp.int32, (16, PIECE), 0)
@@ -323,7 +365,7 @@
                 pr = prob[t]
                 weighted = pr * total
                 coeffs = weighted - pr * jnp.sum(weighted, axis=0, keepdims=True)
-            E[ph, t, y] = coeffs.astype(bf16)
+            E[ph, t, y] = pack_piece(coeffs).astype(bf16)
             for i in range(1, YS):
                 ag_copy(ph, t, i).start()
 
@@ -335,11 +377,14 @@
         def _(t):
             for i in range(1, YS):
                 ag_recv(ph, t, i).wait_recv()
-            e = jnp.concatenate([E[ph, t, o] for o in range(YS)], axis=1)
+            e = jnp.concatenate([spread_piece(E[ph, t, o].astype(f32)) for o in range(YS)], axis=1).astype(bf16)
             at = pl.ds(pl.multiple_of(t * CROWS, CROWS), CROWS)
             for h in range(2):
                 Q[h] = Q[h] + jnp.dot(e, X[h, at], preferred_element_type=f32)
 
+        for h in range(2):
+            Q[h] = fold_rows(Q[h])
+
     def q_copy(ph):
         return rcopy(Q.at[1 - c], Qr.at[ph], q_s.at[ph], q_r.at[ph], sib)
 
@@ -357,12 +402,15 @@
         o = feat_dev(i)
         return rcopy(fe.at[ph, o], fe.at[ph, o], fe_s.at[ph, i], fe_r.at[ph, o], (s, o))
 
+    def chip_sum(ph):
+        q_copy(ph).start()
+        q_copy(ph).wait_recv()
+        return pack(Q[c] + Qr[ph])
+
     @scoped('sums_start')
     def start_sums(ph):
-        q_copy(ph).start()
-        q_copy(ph).wait_recv()
-        ar[ph, s] = pack(Q[c] + Qr[ph])
-        for i in FAR_SAMP:
+        ar[ph, s] = chip_sum(ph)
+        for i in range(1, SAMP):
             ar_copy(ph, i).start()
 
     @scoped('sums_finish')
@@ -372,6 +420,26 @@
         total = ar[ph, 0]
         for o in range(1, SAMP):
             total = total + ar[ph, o]
+        return total
+
+    def last_copy(i):
+        return rcopy(dots.at[s], dots.at[s], ar_s.at[ITERS, i], ar_r.at[ITERS, s], (samp_dev(i), f))
+
+    def last_recv(i):
+        o = samp_dev(i)
+        return rcopy(dots.at[o], dots.at[o], ar_s.at[ITERS, i], ar_r.at[ITERS, o], (o, f))
+
+    @scoped('sums_last')
+    def sums_last(message):
+        dots[s] = message
+        for i in range(1, SAMP):
+            last_copy(i).start()
+        drain(ITERS, False)
+        for i in range(1, SAMP):
+            last_recv(i).wait_recv()
+        total = dots[0]
+        for o in range(1, SAMP):
+            total = total + dots[o]
         return total
 
     @scoped('drain')
@@ -397,19 +465,17 @@
             total = total + fe[ph, o]
         return total
 
-    with jax.named_scope('dwait'):
-        d_recv(0).wait_recv()
     images(0, True)
 
     @scoped('gram_gather')
     def gram_gather():
-        for kb in range(4):
-            for o in range(OFFS[kb], OFFS[kb] + 4 - kb):
+        for m, (start, count) in enumerate(MSGS):
+            for o in range(start, start + count):
                 @pl.when(s != o)
                 def _():
                     gs_recv(o).wait_recv()
             for i in FAR_FEAT:
-                gy_copy(kb, i).start()
+                gy_copy(m, i).start()
 
     gram_gather()
     pieces(0, True)
@@ -454,7 +520,7 @@
     for kb in range(4):
         with jax.named_scope('chol_wait'):
             for i in range(1, FEAT):
-                gy_recv(kb, i).wait_recv()
+                gy_recv(kb + 1 if kb else 0, i).wait_recv()
         with jax.named_scope('chol'):
             FA[...] = gram_block(kb, kb)
             FN[...] = eye
@@ -462,6 +528,9 @@
                 rest_of(kb - 1)
             factor_block(FA, FN)
             V[kb, :, lanes(4 + kb, 5 + kb)] = FN[...]
+            if kb == 0:
+                for i in range(1, FEAT):
+                    gy_recv(1, i).wait_recv()
             if kb < 3:
                 V[kb, :, lanes(kb + 1, kb + 2)] = dot_hi(FN[...], gram_block(kb, kb + 1))
                 add_to(kb, kb + 1, kb + 1, kb + 2)
@@ -568,33 +637,34 @@
     @pl.loop(0, ITERS)
     def _(it):
         ph = it + 1
-        with jax.named_scope('dwait'):
-            d_recv(ph).wait_recv()
         images(ph, False)
         pieces(ph, False)
         collect(ph)
-        start_sums(ph)
-        drain(ph, False)
-        d, r = vec[1], vec[0]
-        q = finish_sums(ph) / NS + RIDGE * d
-        bq = basis_dots(q)
-        tot = exchange(ph, jnp.concatenate(bq + [
-            both(lanes_of(d, q), lanes_of(r, d)),
-            both(lanes_of(r, q), lanes_of(q, q)),
-            both(lanes_of(r, r), zrow),
-            zrow,
-        ], axis=0))
-        lo, hi = halves(tot)
-        step = hi[4:5] / lo[4:5]
-        x = vec[2] + step * d
-        vec[2] = x
 
         @pl.when(it == ITERS - 1)
         def _():
-            out[...] = unpack(x)[:K]
+            d, r = vec[1], vec[0]
+            dq = sums_last(jnp.broadcast_to(lanes_of(d, chip_sum(ITERS)), (8, 128)))[0:1]
+            dq = dq / NS + RIDGE * lanes_of(d, d)
+            lo, hi = halves(exchange(ITERS, jnp.broadcast_to(both(dq, lanes_of(r, d)), (8, 128))))
+            out[...] = unpack(vec[2] + hi[0:1] / lo[0:1] * d)[:K]
 
         @pl.when(it < ITERS - 1)
         def _():
+            start_sums(ph)
+            drain(ph, False)
+            d, r = vec[1], vec[0]
+            q = finish_sums(ph) / NS + RIDGE * d
+            bq = basis_dots(q)
+            tot = exchange(ph, jnp.concatenate(bq + [
+                both(lanes_of(d, q), lanes_of(r, d)),
+                both(lanes_of(r, q), lanes_of(q, q)),
+                both(lanes_of(r, r), zrow),
+                zrow,
+            ], axis=0))
+            lo, hi = halves(tot)
+            step = hi[4:5] / lo[4:5]
+            vec[2] = vec[2] + step * d
             rn = r - step * q
             vec[0] = rn
             pn = prow[...] - step * tot
@@ -616,14 +686,19 @@
         for i in range(1, SAMP):
             gs_copy(i).wait_send()
 
-    for kb in range(4):
+    for m in range(len(MSGS)):
         for i in range(1, FEAT):
-            gy_copy(kb, i).wait_send()
+            gy_copy(m, i).wait_send()
+
+    for i in range(1, SAMP):
+        last_copy(i).wait_send()
 
     @pl.loop(0, ITERS + 1)
     def _(ph):
-        for i in range(1, SAMP):
-            ar_copy(ph, i).wait_send()
+        @pl.when(ph < ITERS)
+        def _():
+            for i in range(1, SAMP):
+                ar_copy(ph, i).wait_send()
         for i in range(1, FEAT):
             fe_copy(ph, i).wait_send()
 
@@ -639,15 +714,16 @@
         V((K * COLS, RANK), f32),
         V((RANK, K * COLS), f32),
         V((PH, 2, 16, COLS), bf16),
-        V((CHUNKS, YS, 16, PIECE), f32),
-        V((CHUNKS, YS, 16, PIECE), bf16),
-        V((CHUNKS, YS, 16, PIECE), f32),
-        V((ITERS, CHUNKS, YS, 16, PIECE), bf16),
+        V((CHUNKS, YS, 8, PWIDE), f32),
+        V((CHUNKS, YS, 8, PWIDE), bf16),
+        V((CHUNKS, YS, 8, PWIDE), f32),
+        V((ITERS, CHUNKS, YS, 8, PWIDE), bf16),
         V((CHUNKS, 16, PIECE), f32),
-        V((PH, CHUNKS, YS, 16, PIECE), bf16),
+        V((PH, CHUNKS, YS, 8, PWIDE), bf16),
         V((2, 16, COLS), f32),
         V((PH, 16, COLS), f32),
-        V((PH, SAMP, 8, 384), f32),
+        V((ITERS, SAMP, 8, 384), f32),
+        V((SAMP, 8, 128), f32),
         V((PH, FEAT, 8, 128), f32),
         V((CHUNKS, 1, PIECE), jnp.int32),
         V((FEAT, 16, 128), f32),
@@ -667,7 +743,7 @@
         dma((PH,)), dma((PH,)), dma((PH,)), dma((PH,)),
         dma((PH, SAMP)), dma((PH, SAMP)), dma((PH, FEAT)), dma((PH, FEAT)),
         dma((FEAT,)), dma((FEAT,)), dma((SAMP,)), dma((SAMP,)),
-        dma((4, FEAT)), dma((4, FEAT)), dma((CHUNKS,)),
+        dma((5, FEAT)), dma((5, FEAT)), dma((CHUNKS,)),
     ]
     step = pl.pallas_call(
         kernel,

time: 122 us -> 116 us (0.951)
  Pallas kernels: 121 us -> 115 us
    pallas_call x1, Pallas kernels: 121 us -> 115 us  [on_device(): pl.pallas_call(kernel, out_shape=jax.ShapeDtypeStruct((K, COLS), f32), in...]
where the time goes in v3:
time: 116 us
  Pallas kernels  115 us (99%)
  local copies, waits for them, and re-layouts  1.32 us (1%)
    pallas_call x1, Pallas kernels, on_device(): pl.pallas_call(kernel, out_shape=jax.ShapeDtypeStruct((K, COLS), f32), in...  115 us

profile of v3, /device:TPU:1, one launch (start us, length us, event | category | flops | bytes accessed | tf_op | source)
XLA Modules:
  0.0 116.0 jit_solution(2572742388247430646)
XLA Ops:
  0.0 114.6 %newton_step.1 = f32[10,256]{1,0:T(8,128)} custom-call(bf16[16384,256]{1,0:T(8,128)(2,1)} %feat.1, s32[16384]{0:T(1024)} %labels.1, f32[10,256]{1,0:T(8,128)} %weights.1, f32[2560,512]{1,0:T(8,128)} %bitcast.2, f32[4,128]{1,0:T(4,128)} %bitcast.3), custom_call_target="tpu_custom_call" | custom-call | tf_op jit(solution)/shard_map/newton_step/pallas_call | solution.py:748
  114.7 1.3 %copy.7 = f32[10,256]{1,0:T(8,128)} copy(f32[10,256]{1,0:T(8,128)} %newton_step.1) | data formatting | bytes 20480

commit v4 on v3

--- a/solution.py
+++ b/solution.py
@@ -18,7 +18,8 @@
 CHUNKS = 4
 CROWS = HALF // CHUNKS
 PIECE = CROWS // YS
-PWIDE = PIECE + 128
+PTILES = PIECE // 128
+PWIDE = PIECE + (PTILES + 3) // 4 * 128
 COLS = 256
 K = 10
 RANK = 512
@@ -70,25 +71,34 @@
 
 def pack_piece(wide):
     low = wide[8:16]
-    last = low[:, :128]
-    for q in range(1, PIECE // 128):
-        last = last + pltpu.roll(low[:, q * 128 : (q + 1) * 128], 2 * q, 0)
-    return jnp.concatenate([wide[:8], last], axis=1)
+    tiles = [wide[:8]]
+    for e in range(0, PTILES, 4):
+        last = low[:, e * 128 : (e + 1) * 128]
+        for q in range(e + 1, min(e + 4, PTILES)):
+            last = last + pltpu.roll(low[:, q * 128 : (q + 1) * 128], 2 * (q - e), 0)
+        tiles.append(last)
+    return jnp.concatenate(tiles, axis=1)
+
+
+def shared_tile(packed, q):
+    at = PIECE + q // 4 * 128
+    return packed[:, at : at + 128]
 
 
 def unpack_piece(packed):
-    last = packed[:, PIECE:]
+    row = rows_of(8)
+    low = []
+    for q in range(PTILES):
+        tile = shared_tile(packed, q)
+        low.append(jnp.where(row < 2, pltpu.roll(tile, 8 - 2 * (q % 4), 0) if q % 4 else tile, 0.0))
+    return jnp.concatenate([packed[:, :PIECE], jnp.concatenate(low, axis=1)], axis=0)
+
+
+def spread_piece(packed):
     row = rows_of(8)
     low = [
-        jnp.where(row < 2, pltpu.roll(last, (8 - 2 * q) % 8, 0) if q else last, 0.0) for q in range(PIECE // 128)
+        jnp.where((row >= 2 * (q % 4)) & (row < 2 * (q % 4) + 2), shared_tile(packed, q), 0.0) for q in range(PTILES)
     ]
-    return jnp.concatenate([packed[:, :PIECE], jnp.concatenate(low, axis=1)], axis=0)
-
-
-def spread_piece(packed):
-    last = packed[:, PIECE:]
-    row = rows_of(8)
-    low = [jnp.where((row >= 2 * q) & (row < 2 * q + 2), last, 0.0) for q in range(PIECE // 128)]
     return jnp.concatenate([packed[:, :PIECE], jnp.concatenate(low, axis=1)], axis=0)
 
 
@@ -163,7 +173,7 @@
 
 def kernel(
     feat, labels, weights, basis, svals, out,
-    X, bst, BT, dB, imgf, imgb, recvg, recvh, prob, E, Q, Qr, ar, dots, fe,
+    X, own, bst, BT, dB, imgf, imgb, recvg, recvh, prob, E, Q, Qr, ar, dots, fe,
     lab, gpart, grecv, gall, V, acc, FA, FN, ccol, tmp, vec, prow, scal,
     sx_own, sx_s, sx_r, s_b, rs_s, rs_r, ag_s, ag_r, q_s, q_r, d_s, d_r,
     ar_s, ar_r, fe_s, fe_r, gf_s, gf_r, gs_s, gs_r, gy_s, gy_r, l_s,
@@ -317,20 +327,17 @@
 
     @scoped('images')
     def images(ph, grad):
-        @pl.loop(0, CHUNKS)
-        def _(t):
-            at = pl.ds(pl.multiple_of(t * CROWS, CROWS), CROWS)
+        for t in range(CHUNKS):
+            at = slice(t * CROWS, (t + 1) * CROWS)
             if grad:
                 x_own(t).wait()
-            img = lax.dot_general(dB[ph, c], X[c, at], NT, preferred_element_type=f32)
-
-            @pl.when(t == 0)
-            def _():
-                d_recv(ph).wait_recv()
-
+            own[t] = lax.dot_general(dB[ph, c], X[c, at], NT, preferred_element_type=f32)
+        d_recv(ph).wait_recv()
+        for t in range(CHUNKS):
+            at = slice(t * CROWS, (t + 1) * CROWS)
             if grad:
                 x_recv(t).wait_recv()
-            img = img + lax.dot_general(dB[ph, 1 - c], X[1 - c, at], NT, preferred_element_type=f32)
+            img = own[t] + lax.dot_general(dB[ph, 1 - c], X[1 - c, at], NT, preferred_element_type=f32)
             for o in range(YS):
                 piece = pack_piece(img[:, o * PIECE : (o + 1) * PIECE])
                 imgf[t, o] = piece
@@ -359,8 +366,8 @@
                 pr = ex / jnp.sum(ex, axis=0, keepdims=True)
                 prob[t] = pr
                 lab_copy(t).wait()
-                own = lab[t]
-                coeffs = pr - jnp.where(row == own, 1.0, 0.0)
+                mine = lab[t]
+                coeffs = pr - jnp.where(row == mine, 1.0, 0.0)
             else:
                 pr = prob[t]
                 weighted = pr * total
@@ -453,11 +460,13 @@
                 rs_copy(ph, t, i, grad).wait_send()
                 ag_copy(ph, t, i).wait_send()
 
-    @scoped('exchange')
-    def exchange(ph, message):
+    def send_sums(ph, message):
         fe[ph, f] = message
         for i in FAR_FEAT:
             fe_copy(ph, i).start()
+
+    @scoped('exchange')
+    def take_sums(ph):
         for i in range(1, FEAT):
             fe_recv(ph, i).wait_recv()
         total = fe[ph, 0]
@@ -465,11 +474,16 @@
             total = total + fe[ph, o]
         return total
 
+    def exchange(ph, message):
+        send_sums(ph, message)
+        return take_sums(ph)
+
     images(0, True)
 
     @scoped('gram_gather')
-    def gram_gather():
-        for m, (start, count) in enumerate(MSGS):
+    def gram_gather(first, last):
+        for m in range(first, last):
+            start, count = MSGS[m]
             for o in range(start, start + count):
                 @pl.when(s != o)
                 def _():
@@ -477,8 +491,9 @@
             for i in FAR_FEAT:
                 gy_copy(m, i).start()
 
-    gram_gather()
+    gram_gather(0, 2)
     pieces(0, True)
+    gram_gather(2, 5)
 
     sv = svals[...]
     low = jnp.min(jnp.min(sv, axis=1, keepdims=True), axis=0, keepdims=True)
@@ -516,28 +531,6 @@
             if k > 0:
                 add_to(k, i, 4, 4 + k)
             add_to(k, i, 4 + k, 5 + k)
-
-    for kb in range(4):
-        with jax.named_scope('chol_wait'):
-            for i in range(1, FEAT):
-                gy_recv(kb + 1 if kb else 0, i).wait_recv()
-        with jax.named_scope('chol'):
-            FA[...] = gram_block(kb, kb)
-            FN[...] = eye
-            if kb > 0:
-                rest_of(kb - 1)
-            factor_block(FA, FN)
-            V[kb, :, lanes(4 + kb, 5 + kb)] = FN[...]
-            if kb == 0:
-                for i in range(1, FEAT):
-                    gy_recv(1, i).wait_recv()
-            if kb < 3:
-                V[kb, :, lanes(kb + 1, kb + 2)] = dot_hi(FN[...], gram_block(kb, kb + 1))
-                add_to(kb, kb + 1, kb + 1, kb + 2)
-        if kb == 1:
-            collect(0)
-            start_sums(0)
-    rest_of(3)
 
     @scoped('basis_dots')
     def basis_dots(packed):
@@ -620,19 +613,44 @@
 
     NS = float(SAMP * ROWS)
     zrow = jnp.zeros((1, 128), f32)
-    res = -(finish_sums(0) * (math.sqrt(F) / NS) + RIDGE * pack(w))
+    for kb in range(4):
+        with jax.named_scope('chol_wait'):
+            for i in range(1, FEAT):
+                gy_recv(kb + 1 if kb else 0, i).wait_recv()
+        with jax.named_scope('chol'):
+            FA[...] = gram_block(kb, kb)
+            FN[...] = eye
+            if kb > 0:
+                rest_of(kb - 1)
+            factor_block(FA, FN)
+            V[kb, :, lanes(4 + kb, 5 + kb)] = FN[...]
+            if kb == 0:
+                for i in range(1, FEAT):
+                    gy_recv(1, i).wait_recv()
+            if kb < 3:
+                V[kb, :, lanes(kb + 1, kb + 2)] = dot_hi(FN[...], gram_block(kb, kb + 1))
+                add_to(kb, kb + 1, kb + 1, kb + 2)
+        if kb == 0:
+            collect(0)
+            start_sums(0)
+        if kb == 2:
+            res = -(finish_sums(0) * (math.sqrt(F) / NS) + RIDGE * pack(w))
+            vec[0] = res
+            send_sums(0, jnp.concatenate(
+                basis_dots(res) + [zrow, zrow, both(lanes_of(res, res), zrow), zrow], axis=0
+            ))
+    rest_of(3)
+
     drain(0, True)
-    p0 = basis_dots(res)
-    tot = exchange(0, jnp.concatenate(p0 + [zrow, zrow, both(lanes_of(res, res), zrow), zrow], axis=0))
+    tot = take_sums(0)
     lo, hi = halves(tot)
     y_rows, py = inner_part([tot[i : i + 1] for i in range(4)])
     rr = lo[6:7]
     prow[...] = tot
-    vec[0] = res
     vec[2] = jnp.zeros((8, 384), f32)
     scal[0:1, :] = jnp.broadcast_to(rr, (1, 128))
     scal[1:2, :] = jnp.broadcast_to(rr + py, (1, 128))
-    set_direction(1, res + basis_apply(y_rows))
+    set_direction(1, vec[0] + basis_apply(y_rows))
 
     @pl.loop(0, ITERS)
     def _(it):
@@ -711,6 +729,7 @@
     PH = ITERS + 1
     scratch = [
         V((2, HALF, COLS), bf16),
+        V((CHUNKS, 16, CROWS), f32),
         V((K * COLS, RANK), f32),
         V((RANK, K * COLS), f32),
         V((PH, 2, 16, COLS), bf16),

time: 116 us -> 112 us (0.966)
  Pallas kernels: 115 us -> 110 us
    pallas_call x1, Pallas kernels: 115 us -> 110 us  [on_device(): pl.pallas_call(kernel, out_shape=jax.ShapeDtypeStruct((K, COLS), f32), in...]
where the time goes in v4:
time: 112 us
  Pallas kernels  110 us (98%)
  local copies, waits for them, and re-layouts  1.32 us (1%)
    pallas_call x1, Pallas kernels, on_device(): pl.pallas_call(kernel, out_shape=jax.ShapeDtypeStruct((K, COLS), f32), in...  110 us

profile of v4, /device:TPU:1, one launch (start us, length us, event | category | flops | bytes accessed | tf_op | source)
XLA Modules:
  0.0 111.7 jit_solution(5997541528545599414)
XLA Ops:
  0.0 110.3 %newton_step.1 = f32[10,256]{1,0:T(8,128)} custom-call(bf16[16384,256]{1,0:T(8,128)(2,1)} %feat.1, s32[16384]{0:T(1024)} %labels.1, f32[10,256]{1,0:T(8,128)} %weights.1, f32[2560,512]{1,0:T(8,128)} %bitcast.2, f32[4,128]{1,0:T(4,128)} %bitcast.3), custom_call_target="tpu_custom_call" | custom-call | tf_op jit(solution)/shard_map/newton_step/pallas_call | solution.py:767
  110.3 1.3 %copy.7 = f32[10,256]{1,0:T(8,128)} copy(f32[10,256]{1,0:T(8,128)} %newton_step.1) | data formatting | bytes 20480

commit v5 on v4

--- a/solution.py
+++ b/solution.py
@@ -193,6 +193,15 @@
     def y_dev(i):
         return lax.rem(y + i, YS)
 
+    def slot(o, me, n):
+        return lax.rem(o - me + n, n)
+
+    def in_order(ref, me, n):
+        total = ref[slot(0, me, n)]
+        for o in range(1, n):
+            total = total + ref[slot(o, me, n)]
+        return total
+
     for k in range(K):
         pltpu.make_async_copy(basis.at[pl.ds(k * COLS, COLS)], bst.at[pl.ds(k * COLS, COLS)], s_b.at[k]).start()
 
@@ -206,11 +215,14 @@
         return pltpu.make_async_copy(feat.at[own_rows(t)], X.at[c, pl.ds(t * CROWS, CROWS)], sx_own.at[t])
 
     def x_send(t):
-        return rcopy(feat.at[sib_rows(t)], X.at[c, pl.ds(t * CROWS, CROWS)], sx_s.at[t], sx_r.at[t], sib)
+        return rcopy(feat.at[sib_rows(t)], X.at[c, pl.ds(t * CROWS, CROWS)], sx_s.at[0], sx_r.at[t], sib)
 
     def x_recv(t):
         dst = X.at[1 - c, pl.ds(t * CROWS, CROWS)]
-        return rcopy(dst, dst, sx_s.at[t], sx_r.at[t], sib)
+        return rcopy(dst, dst, sx_s.at[0], sx_r.at[t], sib)
+
+    def x_sent():
+        return rcopy(X.at[c], X.at[c], sx_s.at[0], sx_r.at[0], sib)
 
     def lab_copy(t):
         start = pl.multiple_of(c * HALF + t * CROWS + y * PIECE, PIECE)
@@ -218,10 +230,10 @@
 
 
     def d_copy(ph):
-        return rcopy(dB.at[ph, c], dB.at[ph, c], d_s.at[ph], d_r.at[ph], sib)
+        return rcopy(dB.at[ph, c], dB.at[ph, c], d_s.at[0], d_r.at[0], sib)
 
     def d_recv(ph):
-        return rcopy(dB.at[ph, 1 - c], dB.at[ph, 1 - c], d_s.at[ph], d_r.at[ph], sib)
+        return rcopy(dB.at[ph, 1 - c], dB.at[ph, 1 - c], d_s.at[0], d_r.at[0], sib)
 
     barrier = pltpu.get_barrier_semaphore()
     for i in range(1, FEAT):
@@ -262,25 +274,29 @@
 
     def gf_copy(i):
         o = feat_dev(i)
-        return rcopy(gpart.at[o], grecv.at[f], gf_s.at[i], gf_r.at[f], (s, o))
-
-    def gf_recv(i):
-        o = feat_dev(i)
-        return rcopy(grecv.at[o], grecv.at[o], gf_s.at[i], gf_r.at[o], (s, o))
+        return rcopy(gpart.at[o], grecv.at[FEAT - i], gf_s.at[0], gf_r.at[0], (s, o))
+
+    def gf_all():
+        every = grecv.at[pl.ds(1, FEAT - 1)]
+        return rcopy(every, every, gf_s.at[0], gf_r.at[0], sib)
 
     def gs_copy(i):
-        return rcopy(gall.at[f, s], gall.at[f, s], gs_s.at[i], gs_r.at[s], (samp_dev(i), f))
+        return rcopy(gall.at[0, s], gall.at[0, s], gs_s.at[0], gs_r.at[s], (samp_dev(i), f))
+
+    def gs_sent():
+        every = gall.at[0, pl.ds(0, SAMP - 1)]
+        return rcopy(every, every, gs_s.at[0], gs_r.at[0], sib)
 
     def gs_recv(o):
-        return rcopy(gall.at[f, o], gall.at[f, o], gs_s.at[0], gs_r.at[o], (o, f))
+        return rcopy(gall.at[0, o], gall.at[0, o], gs_s.at[0], gs_r.at[o], (o, f))
 
     def gy_copy(m, i):
         at = pl.ds(*MSGS[m])
-        return rcopy(gall.at[f, at], gall.at[f, at], gy_s.at[m, i], gy_r.at[m, f], (s, feat_dev(i)))
-
-    def gy_recv(m, i):
-        at, o = pl.ds(*MSGS[m]), feat_dev(i)
-        return rcopy(gall.at[o, at], gall.at[o, at], gy_s.at[m, i], gy_r.at[m, o], (s, o))
+        return rcopy(gall.at[0, at], gall.at[FEAT - i, at], gy_s.at[m], gy_r.at[m], (s, feat_dev(i)))
+
+    def gy_all(m):
+        every = gall.at[pl.ds(1, FEAT - 1), pl.ds(*MSGS[m])]
+        return rcopy(every, every, gy_s.at[m], gy_r.at[m], sib)
 
     with jax.named_scope('barrier'):
         pl.semaphore_wait(barrier, FEAT - 1 + SAMP - 1)
@@ -294,44 +310,43 @@
     for t in range(CHUNKS):
         x_send(t).start()
 
-    @pl.when(s < 10)
-    @scoped('gram_sum')
-    def _():
-        for i in range(1, FEAT):
-            gf_recv(i).wait_recv()
-        grecv[f] = gpart[f]
-        total = grecv[0]
-        for o in range(1, FEAT):
-            total = total + grecv[o]
-        gall[f, s] = total
-        for i in FAR_SAMP:
-            gs_copy(i).start()
-
     def rs_copy(ph, t, i, grad):
         o = y_dev(i)
         src = imgf.at[t, o] if grad else imgb.at[t, o]
-        dst = recvg.at[t, y] if grad else recvh.at[ph - 1, t, y]
-        return rcopy(src, dst, rs_s.at[ph, t, i], rs_r.at[ph, t, y], (s, CORES * o + c))
-
-    def rs_recv(ph, t, i, grad):
-        o = y_dev(i)
-        dst = recvg.at[t, o] if grad else recvh.at[ph - 1, t, o]
-        return rcopy(dst, dst, rs_s.at[ph, t, i], rs_r.at[ph, t, o], (s, CORES * o + c))
+        dst = recvg.at[t, YS - i] if grad else recvh.at[ph - 1, t, YS - i]
+        return rcopy(src, dst, rs_s.at[0], rs_r.at[t], (s, CORES * o + c))
+
+    def rs_all(ph, t, grad):
+        every = recvg.at[t, pl.ds(1, YS - 1)] if grad else recvh.at[ph - 1, t, pl.ds(1, YS - 1)]
+        return rcopy(every, every, rs_s.at[0], rs_r.at[t], sib)
+
+    def rs_sent(grad):
+        every = imgf.at[pl.ds(0, YS - 1)] if grad else imgb.at[pl.ds(0, YS - 1)]
+        return rcopy(every, every, rs_s.at[0], rs_r.at[0], sib)
 
     def ag_copy(ph, t, i):
-        return rcopy(E.at[ph, t, y], E.at[ph, t, y], ag_s.at[ph, t, i], ag_r.at[ph, t, y], (s, CORES * y_dev(i) + c))
-
-    def ag_recv(ph, t, i):
-        o = y_dev(i)
-        return rcopy(E.at[ph, t, o], E.at[ph, t, o], ag_s.at[ph, t, i], ag_r.at[ph, t, o], (s, CORES * o + c))
-
-    @scoped('images')
-    def images(ph, grad):
+        return rcopy(E.at[ph, t, 0], E.at[ph, t, YS - i], ag_s.at[0], ag_r.at[t], (s, CORES * y_dev(i) + c))
+
+    def ag_all(ph, t):
+        every = E.at[ph, t, pl.ds(1, YS - 1)]
+        return rcopy(every, every, ag_s.at[0], ag_r.at[t], sib)
+
+    def ag_sent(ph):
+        every = E.at[ph, pl.ds(0, YS - 1)]
+        return rcopy(every, every, ag_s.at[0], ag_r.at[0], sib)
+
+    @scoped('own_images')
+    def own_images(ph, grad):
         for t in range(CHUNKS):
             at = slice(t * CROWS, (t + 1) * CROWS)
             if grad:
                 x_own(t).wait()
             own[t] = lax.dot_general(dB[ph, c], X[c, at], NT, preferred_element_type=f32)
+
+    @scoped('images')
+    def images(ph, grad):
+        if not grad:
+            own_images(ph, False)
         d_recv(ph).wait_recv()
         for t in range(CHUNKS):
             at = slice(t * CROWS, (t + 1) * CROWS)
@@ -351,11 +366,9 @@
         @pl.loop(0, CHUNKS)
         def _(t):
             total = imgf[t, y]
+            rs_all(ph, t, grad).wait_recv()
             for i in range(1, YS):
-                rs_recv(ph, t, i, grad).wait_recv()
-            for i in range(1, YS):
-                o = y_dev(i)
-                total = total + (recvg[t, o] if grad else recvh[ph - 1, t, o].astype(f32))
+                total = total + (recvg[t, i] if grad else recvh[ph - 1, t, i].astype(f32))
             total = unpack_piece(total)
             if grad:
                 logits = total / math.sqrt(F)
@@ -372,7 +385,7 @@
                 pr = prob[t]
                 weighted = pr * total
                 coeffs = weighted - pr * jnp.sum(weighted, axis=0, keepdims=True)
-            E[ph, t, y] = pack_piece(coeffs).astype(bf16)
+            E[ph, t, 0] = pack_piece(coeffs).astype(bf16)
             for i in range(1, YS):
                 ag_copy(ph, t, i).start()
 
@@ -382,9 +395,8 @@
 
         @pl.loop(0, CHUNKS)
         def _(t):
-            for i in range(1, YS):
-                ag_recv(ph, t, i).wait_recv()
-            e = jnp.concatenate([spread_piece(E[ph, t, o].astype(f32)) for o in range(YS)], axis=1).astype(bf16)
+            ag_all(ph, t).wait_recv()
+            e = jnp.concatenate([spread_piece(E[ph, t, slot(o, y, YS)].astype(f32)) for o in range(YS)], axis=1).astype(bf16)
             at = pl.ds(pl.multiple_of(t * CROWS, CROWS), CROWS)
             for h in range(2):
                 Q[h] = Q[h] + jnp.dot(e, X[h, at], preferred_element_type=f32)
@@ -393,21 +405,21 @@
             Q[h] = fold_rows(Q[h])
 
     def q_copy(ph):
-        return rcopy(Q.at[1 - c], Qr.at[ph], q_s.at[ph], q_r.at[ph], sib)
+        return rcopy(Q.at[1 - c], Qr.at[ph], q_s.at[0], q_r.at[0], sib)
 
     def ar_copy(ph, i):
-        return rcopy(ar.at[ph, s], ar.at[ph, s], ar_s.at[ph, i], ar_r.at[ph, s], (samp_dev(i), f))
-
-    def ar_recv(ph, i):
-        o = samp_dev(i)
-        return rcopy(ar.at[ph, o], ar.at[ph, o], ar_s.at[ph, i], ar_r.at[ph, o], (o, f))
+        return rcopy(ar.at[ph, 0], ar.at[ph, SAMP - i], ar_s.at[ph], ar_r.at[ph], (samp_dev(i), f))
+
+    def ar_all(ph):
+        every = ar.at[ph, pl.ds(1, SAMP - 1)]
+        return rcopy(every, every, ar_s.at[ph], ar_r.at[ph], sib)
 
     def fe_copy(ph, i):
-        return rcopy(fe.at[ph, f], fe.at[ph, f], fe_s.at[ph, i], fe_r.at[ph, f], (s, feat_dev(i)))
-
-    def fe_recv(ph, i):
-        o = feat_dev(i)
-        return rcopy(fe.at[ph, o], fe.at[ph, o], fe_s.at[ph, i], fe_r.at[ph, o], (s, o))
+        return rcopy(fe.at[ph, 0], fe.at[ph, FEAT - i], fe_s.at[ph], fe_r.at[ph], (s, feat_dev(i)))
+
+    def fe_all(ph):
+        every = fe.at[ph, pl.ds(1, FEAT - 1)]
+        return rcopy(every, every, fe_s.at[ph], fe_r.at[ph], sib)
 
     def chip_sum(ph):
         q_copy(ph).start()
@@ -416,67 +428,78 @@
 
     @scoped('sums_start')
     def start_sums(ph):
-        ar[ph, s] = chip_sum(ph)
+        ar[ph, 0] = chip_sum(ph)
         for i in range(1, SAMP):
             ar_copy(ph, i).start()
 
     @scoped('sums_finish')
     def finish_sums(ph):
-        for i in range(1, SAMP):
-            ar_recv(ph, i).wait_recv()
-        total = ar[ph, 0]
-        for o in range(1, SAMP):
-            total = total + ar[ph, o]
-        return total
+        ar_all(ph).wait_recv()
+        return in_order(ar.at[ph], s, SAMP)
 
     def last_copy(i):
-        return rcopy(dots.at[s], dots.at[s], ar_s.at[ITERS, i], ar_r.at[ITERS, s], (samp_dev(i), f))
-
-    def last_recv(i):
-        o = samp_dev(i)
-        return rcopy(dots.at[o], dots.at[o], ar_s.at[ITERS, i], ar_r.at[ITERS, o], (o, f))
+        return rcopy(dots.at[0], dots.at[SAMP - i], ar_s.at[ITERS], ar_r.at[ITERS], (samp_dev(i), f))
+
+    def last_all():
+        every = dots.at[pl.ds(1, SAMP - 1)]
+        return rcopy(every, every, ar_s.at[ITERS], ar_r.at[ITERS], sib)
 
     @scoped('sums_last')
     def sums_last(message):
-        dots[s] = message
+        dots[0] = message
         for i in range(1, SAMP):
             last_copy(i).start()
         drain(ITERS, False)
-        for i in range(1, SAMP):
-            last_recv(i).wait_recv()
-        total = dots[0]
-        for o in range(1, SAMP):
-            total = total + dots[o]
-        return total
+        drain_sums(ITERS - 2)
+        last_all().wait_recv()
+        return in_order(dots, s, SAMP)
 
     @scoped('drain')
     def drain(ph, grad):
         d_copy(ph).wait_send()
         q_copy(ph).wait_send()
-
-        @pl.loop(0, CHUNKS)
-        def _(t):
-            for i in range(1, YS):
-                rs_copy(ph, t, i, grad).wait_send()
-                ag_copy(ph, t, i).wait_send()
+        rs_sent(grad).wait_send()
+        ag_sent(ph).wait_send()
+
+    def drain_setup():
+        x_sent().wait_send()
+
+        @pl.when(s < 10)
+        def _():
+            gf_all().wait_send()
+            gs_sent().wait_send()
+
+        for m in range(len(MSGS)):
+            gy_all(m).wait_send()
+
+    def drain_sums(ph):
+        ar_all(ph).wait_send()
+        fe_all(ph).wait_send()
 
     def send_sums(ph, message):
-        fe[ph, f] = message
+        fe[ph, 0] = message
         for i in FAR_FEAT:
             fe_copy(ph, i).start()
 
     @scoped('exchange')
     def take_sums(ph):
-        for i in range(1, FEAT):
-            fe_recv(ph, i).wait_recv()
-        total = fe[ph, 0]
-        for o in range(1, FEAT):
-            total = total + fe[ph, o]
-        return total
+        fe_all(ph).wait_recv()
+        return in_order(fe.at[ph], f, FEAT)
 
     def exchange(ph, message):
         send_sums(ph, message)
         return take_sums(ph)
+
+    own_images(0, True)
+
+    @pl.when(s < 10)
+    @scoped('gram_sum')
+    def _():
+        gf_all().wait_recv()
+        grecv[0] = gpart[f]
+        gall[0, s] = in_order(grecv, f, FEAT)
+        for i in FAR_SAMP:
+            gs_copy(i).start()
 
     images(0, True)
 
@@ -509,7 +532,7 @@
         return lax.dot_general(a, b, dims, precision=HI, preferred_element_type=f32)
 
     def gram_block(k, l):
-        blk = jnp.concatenate([gall[o, OFFS[k] + l - k] for o in range(FEAT)], axis=0)
+        blk = jnp.concatenate([gall[slot(o, f, FEAT), OFFS[k] + l - k] for o in range(FEAT)], axis=0)
         return blk if k == 0 else blk - acc[k, :, lanes(l, l + 1)]
 
     def add_to(k, i, a, b):
@@ -615,8 +638,7 @@
     zrow = jnp.zeros((1, 128), f32)
     for kb in range(4):
         with jax.named_scope('chol_wait'):
-            for i in range(1, FEAT):
-                gy_recv(kb + 1 if kb else 0, i).wait_recv()
+            gy_all(kb + 1 if kb else 0).wait_recv()
         with jax.named_scope('chol'):
             FA[...] = gram_block(kb, kb)
             FN[...] = eye
@@ -625,8 +647,7 @@
             factor_block(FA, FN)
             V[kb, :, lanes(4 + kb, 5 + kb)] = FN[...]
             if kb == 0:
-                for i in range(1, FEAT):
-                    gy_recv(1, i).wait_recv()
+                gy_all(1).wait_recv()
             if kb < 3:
                 V[kb, :, lanes(kb + 1, kb + 2)] = dot_hi(FN[...], gram_block(kb, kb + 1))
                 add_to(kb, kb + 1, kb + 1, kb + 2)
@@ -664,13 +685,26 @@
             d, r = vec[1], vec[0]
             dq = sums_last(jnp.broadcast_to(lanes_of(d, chip_sum(ITERS)), (8, 128)))[0:1]
             dq = dq / NS + RIDGE * lanes_of(d, d)
-            lo, hi = halves(exchange(ITERS, jnp.broadcast_to(both(dq, lanes_of(r, d)), (8, 128))))
-            out[...] = unpack(vec[2] + hi[0:1] / lo[0:1] * d)[:K]
+            send_sums(ITERS, jnp.broadcast_to(both(dq, lanes_of(r, d)), (8, 128)))
+            drain_sums(ITERS - 1)
+            last_all().wait_send()
+            lo, hi = halves(take_sums(ITERS))
+            with jax.named_scope('out'):
+                out[...] = unpack(vec[2] + hi[0:1] / lo[0:1] * d)[:K]
 
         @pl.when(it < ITERS - 1)
         def _():
             start_sums(ph)
             drain(ph, False)
+
+            @pl.when(it == 0)
+            def _():
+                drain_setup()
+
+            @pl.when(it > 0)
+            def _():
+                drain_sums(ph - 2)
+
             d, r = vec[1], vec[0]
             q = finish_sums(ph) / NS + RIDGE * d
             bq = basis_dots(q)
@@ -694,31 +728,8 @@
             scal[1:2, :] = jnp.broadcast_to(new, (1, 128))
             set_direction(ph + 1, rn + basis_apply(y_rows) + beta * d)
 
-    for t in range(CHUNKS):
-        x_send(t).wait_send()
-
-    @pl.when(s < 10)
-    def _():
-        for i in range(1, FEAT):
-            gf_copy(i).wait_send()
-        for i in range(1, SAMP):
-            gs_copy(i).wait_send()
-
-    for m in range(len(MSGS)):
-        for i in range(1, FEAT):
-            gy_copy(m, i).wait_send()
-
-    for i in range(1, SAMP):
-        last_copy(i).wait_send()
-
-    @pl.loop(0, ITERS + 1)
-    def _(ph):
-        @pl.when(ph < ITERS)
-        def _():
-            for i in range(1, SAMP):
-                ar_copy(ph, i).wait_send()
-        for i in range(1, FEAT):
-            fe_copy(ph, i).wait_send()
+    with jax.named_scope('last_waits'):
+        fe_all(ITERS).wait_send()
 
 
 def on_device(features, labels, weights, sketch_basis, sketch_values):
@@ -757,12 +768,12 @@
         V((3, 8, 384), f32),
         V((8, 128), f32),
         V((8, 128), f32),
-        dma((CHUNKS,)), dma((CHUNKS,)), dma((CHUNKS,)), dma((K,)),
-        dma((PH, CHUNKS, YS)), dma((PH, CHUNKS, YS)), dma((PH, CHUNKS, YS)), dma((PH, CHUNKS, YS)),
+        dma((CHUNKS,)), dma((1,)), dma((CHUNKS,)), dma((K,)),
+        dma((1,)), dma((CHUNKS,)), dma((1,)), dma((CHUNKS,)),
+        dma((1,)), dma((1,)), dma((1,)), dma((1,)),
         dma((PH,)), dma((PH,)), dma((PH,)), dma((PH,)),
-        dma((PH, SAMP)), dma((PH, SAMP)), dma((PH, FEAT)), dma((PH, FEAT)),
-        dma((FEAT,)), dma((FEAT,)), dma((SAMP,)), dma((SAMP,)),
-        dma((5, FEAT)), dma((5, FEAT)), dma((CHUNKS,)),
+        dma((1,)), dma((1,)), dma((1,)), dma((10,)),
+        dma((len(MSGS),)), dma((len(MSGS),)), dma((CHUNKS,)),
     ]
     step = pl.pallas_call(
         kernel,

time: 112 us -> 106 us (0.946)
  Pallas kernels: 110 us -> 104 us
    pallas_call x1, Pallas kernels: 110 us -> 104 us  [on_device(): pl.pallas_call(kernel, out_shape=jax.ShapeDtypeStruct((K, COLS), f32), in...]
where the time goes in v5:
time: 106 us; the launch traced here: 105 us
  Pallas kernels  104 us (98%)
  local copies, waits for them, and re-layouts  1.32 us (1%)
    pallas_call x1, Pallas kernels, on_device(): pl.pallas_call(kernel, out_shape=jax.ShapeDtypeStruct((K, COLS), f32), in...  104 us

profile of v5, /device:TPU:1, one launch (start us, length us, event | category | flops | bytes accessed | tf_op | source)
XLA Modules:
  0.0 105.5 jit_solution(517544099436590012)
XLA Ops:
  0.0 104.1 %newton_step.1 = f32[10,256]{1,0:T(8,128)} custom-call(bf16[16384,256]{1,0:T(8,128)(2,1)} %feat.1, s32[16384]{0:T(1024)} %labels.1, f32[10,256]{1,0:T(8,128)} %weights.1, f32[2560,512]{1,0:T(8,128)} %bitcast.2, f32[4,128]{1,0:T(4,128)} %bitcast.3), custom_call_target="tpu_custom_call" | custom-call | tf_op jit(solution)/shard_map/newton_step/pallas_call | solution.py:778
  104.1 1.3 %copy.7 = f32[10,256]{1,0:T(8,128)} copy(f32[10,256]{1,0:T(8,128)} %newton_step.1) | data formatting | bytes 20480

commit v6 on v5

--- a/solution.py
+++ b/solution.py
@@ -358,7 +358,7 @@
                 imgf[t, o] = piece
                 if not grad:
                     imgb[t, o] = piece.astype(bf16)
-            for i in range(1, YS):
+            for i in (2, 1, 3):
                 rs_copy(ph, t, i, grad).start()
 
     @scoped('pieces')
@@ -386,7 +386,7 @@
                 weighted = pr * total
                 coeffs = weighted - pr * jnp.sum(weighted, axis=0, keepdims=True)
             E[ph, t, 0] = pack_piece(coeffs).astype(bf16)
-            for i in range(1, YS):
+            for i in (2, 1, 3):
                 ag_copy(ph, t, i).start()
 
     @scoped('collect')

time: 106 us -> 105 us (level)
  no operation moved by 1% of the time
where the time goes in v6:
time: 105 us
  Pallas kernels  103 us (98%)
  local copies, waits for them, and re-layouts  1.32 us (1%)
    pallas_call x1, Pallas kernels, on_device(): pl.pallas_call(kernel, out_shape=jax.ShapeDtypeStruct((K, COLS), f32), in...  103 us

profile of v6, /device:TPU:1, one launch (start us, length us, event | category | flops | bytes accessed | tf_op | source)
XLA Modules:
  0.0 104.7 jit_solution(9846714671968142505)
XLA Ops:
  0.0 103.4 %newton_step.1 = f32[10,256]{1,0:T(8,128)} custom-call(bf16[16384,256]{1,0:T(8,128)(2,1)} %feat.1, s32[16384]{0:T(1024)} %labels.1, f32[10,256]{1,0:T(8,128)} %weights.1, f32[2560,512]{1,0:T(8,128)} %bitcast.2, f32[4,128]{1,0:T(4,128)} %bitcast.3), custom_call_target="tpu_custom_call" | custom-call | tf_op jit(solution)/shard_map/newton_step/pallas_call | solution.py:778
  103.4 1.3 %copy.7 = f32[10,256]{1,0:T(8,128)} copy(f32[10,256]{1,0:T(8,128)} %newton_step.1) | data formatting | bytes 20480

commit v7 on v6

--- a/solution.py
+++ b/solution.py
@@ -202,6 +202,12 @@
             total = total + ref[slot(o, me, n)]
         return total
 
+    barrier = pltpu.get_barrier_semaphore()
+    for i in FAR_SAMP:
+        pl.semaphore_signal(barrier, inc=1, device_id=(samp_dev(i), f), device_id_type=pl.DeviceIdType.MESH)
+    for i in FAR_FEAT:
+        pl.semaphore_signal(barrier, inc=1, device_id=(s, feat_dev(i)), device_id_type=pl.DeviceIdType.MESH)
+
     for k in range(K):
         pltpu.make_async_copy(basis.at[pl.ds(k * COLS, COLS)], bst.at[pl.ds(k * COLS, COLS)], s_b.at[k]).start()
 
@@ -234,12 +240,6 @@
 
     def d_recv(ph):
         return rcopy(dB.at[ph, 1 - c], dB.at[ph, 1 - c], d_s.at[0], d_r.at[0], sib)
-
-    barrier = pltpu.get_barrier_semaphore()
-    for i in range(1, FEAT):
-        pl.semaphore_signal(barrier, inc=1, device_id=(s, feat_dev(i)), device_id_type=pl.DeviceIdType.MESH)
-    for i in range(1, SAMP):
-        pl.semaphore_signal(barrier, inc=1, device_id=(samp_dev(i), f), device_id_type=pl.DeviceIdType.MESH)
 
     w = jnp.concatenate([weights[...], jnp.zeros((16 - K, COLS), f32)], axis=0)
     dB[0, c] = w.astype(bf16)

time: 105 us -> 105 us (level)
  no operation moved by 1% of the time
where the time goes in v7:
time: 105 us
  Pallas kernels  103 us (98%)
  local copies, waits for them, and re-layouts  1.32 us (1%)
    pallas_call x1, Pallas kernels, on_device(): pl.pallas_call(kernel, out_shape=jax.ShapeDtypeStruct((K, COLS), f32), in...  103 us

profile of v7, /device:TPU:1, one launch (start us, length us, event | category | flops | bytes accessed | tf_op | source)
XLA Modules:
  0.0 104.8 jit_solution(11709919870922208786)
XLA Ops:
  0.0 103.5 %newton_step.1 = f32[10,256]{1,0:T(8,128)} custom-call(bf16[16384,256]{1,0:T(8,128)(2,1)} %feat.1, s32[16384]{0:T(1024)} %labels.1, f32[10,256]{1,0:T(8,128)} %weights.1, f32[2560,512]{1,0:T(8,128)} %bitcast.2, f32[4,128]{1,0:T(4,128)} %bitcast.3), custom_call_target="tpu_custom_call" | custom-call | tf_op jit(solution)/shard_map/newton_step/pallas_call | solution.py:778
  103.5 1.3 %copy.7 = f32[10,256]{1,0:T(8,128)} copy(f32[10,256]{1,0:T(8,128)} %newton_step.1) | data formatting | bytes 20480
